TPU v7x, 256 devices: a whole 4x4x8 slice. The times are simulated.
256 devices in a mesh: seq: 32 (over y, z), head: 8 (over x, core).
Axes of the slice: x: 4, y: 4, z: 8, core: 2. Of those that a mesh axis runs over, the one named last changes fastest.
Arguments:
- tokens: bfloat16 [12288, 4096], P('seq', 'head'), may hold values from -6 to 6
- norm_gain: float32 [4096], replicated, may hold values from 0.25 to 1.75
- w_in: bfloat16 [4096, 8, 2304], P('seq', 'head'), may hold values from -0.09375 to 0.09375
- w_dt: bfloat16 [4096, 128], P('seq', 'head'), may hold values from -0.09375 to 0.09375
- dt_bias: float32 [128], P('head'), may hold values from -3 to -1
- a_log: float32 [128], P('head'), may hold values from -11 to -1
- d_skip: float32 [128], P('head'), may hold values from 0.5 to 1.5
- conv_w: float32 [4, 8, 1280], P(None, 'head'), may hold values from -0.5 to 0.5
- conv_b: float32 [8, 1280], P('head'), may hold values from -0.5 to 0.5
- gate_gain: float32 [8, 1024], P('head'), may hold values from 0.25 to 1.75
- w_out: bfloat16 [8, 1024, 4096], P('head'), may hold values from -0.09375 to 0.09375
Outputs:
- mixed: bfloat16 [12288, 4096], P('seq', 'head')
All inputs are finite; a program needn't handle non-finite values.
Results may differ from a plain program's by a relative error of at most 0.018.
Values may be sent and summed in bfloat16 or wider, within the bound.
A program may use at most 128 MiB of HBM per device.

v0:
```python
from functools import partial

import jax
import jax.numpy as jnp
from jax import lax
from jax.sharding import Mesh
from jax.sharding import PartitionSpec as P

STRETCH = 128
SEQ = ("seq_0", "seq_1")


EPS = 1e-05
HIGHEST = lax.Precision.HIGHEST


def from_behind(shard, axis, by):
    count = lax.axis_size(axis)
    pairs = [(i, i + by) for i in range(count) if 0 <= i + by < count]
    return lax.ppermute(shard, axis, pairs)


def sent_together(arrays, axis, dim, along):
    both = jnp.concatenate(arrays, axis=along)
    result, at, gathered = (lax.all_gather(both, axis, axis=dim, tiled=True), 0, [])
    for a in arrays:
        gathered.append(lax.slice_in_dim(result, at, at + a.shape[along], axis=along))
        at += a.shape[along]
    return tuple(gathered)


def neutral_like(shard, identity):
    return jax.tree.map(
        lambda part, zero: jnp.zeros_like(part) + jnp.asarray(zero, part.dtype), shard, identity
    )


def entering(shard, axes, combine, identity):
    before = start = neutral_like(shard, identity)
    running = shard
    for axis in reversed(axes):
        count, index = (lax.axis_size(axis), lax.axis_index(axis))
        pieces = jax.tree.map(
            lambda part, kind: lax.all_gather(part.astype(kind), axis),
            running,
            (jnp.bfloat16, jnp.bfloat16),
        )
        inside, running = (start, start)
        for k in range(count):
            passed = k < index
            running = combine(
                running, jax.tree.map(lambda part, own: part[k].astype(own.dtype), pieces, shard)
            )
            inside = jax.tree.map(lambda new, old: jnp.where(passed, new, old), running, inside)
        before = combine(inside, before)
    return before


def normalize(values, gain):
    squares = jnp.mean(values * values, axis=-1, keepdims=True)
    return values * lax.rsqrt(squares + EPS) * gain


def state_block(inputs, step_size, log_decay, in_map, out_map, block_len):
    length = inputs.shape[0]
    stretch_count = length // block_len
    head_count = inputs.shape[1]
    head_size = inputs.shape[2]
    state_size = in_map.shape[1]
    shaped = (
        inputs.reshape(stretch_count, block_len, head_count, head_size),
        step_size.reshape(stretch_count, block_len, head_count),
        log_decay.reshape(stretch_count, block_len, head_count),
        in_map.reshape(stretch_count, block_len, state_size),
        out_map.reshape(stretch_count, block_len, state_size),
    )
    causal = jnp.arange(block_len)[:, None] >= jnp.arange(block_len)[None, :]

    def advance(state_now, pieces):
        stretch_in, stretch_step, stretch_log, stretch_b, stretch_c = pieces
        cumulative = jnp.cumsum(stretch_log, axis=0)
        gap_log = cumulative[:, None, :] - cumulative[None, :, :]
        decays = jnp.where(
            causal[:, :, None], jnp.exp(jnp.where(causal[:, :, None], gap_log, 0.0)), 0.0
        )
        scores = jnp.dot(stretch_c, stretch_b.T, preferred_element_type=jnp.float32)
        wide_c = stretch_c.astype(jnp.float32)
        wide_b = stretch_b.astype(jnp.float32)
        weights = scores[:, :, None] * decays * stretch_step[None, :, :]
        within = jnp.einsum("ijh,jhp->ihp", weights, stretch_in, precision=HIGHEST)
        across = jnp.exp(cumulative)[:, :, None] * jnp.einsum(
            "in,hpn->ihp", wide_c, state_now, precision=HIGHEST
        )
        to_end = jnp.exp(cumulative[-1][None, :] - cumulative) * stretch_step
        fresh_state = jnp.einsum("jh,jhp,jn->hpn", to_end, stretch_in, wide_b, precision=HIGHEST)
        state_next = jnp.exp(cumulative[-1])[:, None, None] * state_now + fresh_state
        return (state_next, within + across)

    start_state = jnp.zeros((head_count, head_size, state_size), jnp.float32)
    final, outputs = lax.scan(advance, start_state, shaped)
    return (outputs.reshape(length, head_count, head_size), final)


def link_states(earlier, later):
    return (earlier[0] + later[0], jnp.exp(later[0])[:, :, None, None] * earlier[1] + later[1])


def body(tokens, norm_gain, w_in, w_dt, dt_bias, a_log, d_skip, conv_w, conv_b, gate_gain, w_out):
    local_rows = tokens.shape[0]
    kernel_len = conv_w.shape[0]
    groups, group_width = gate_gain.shape
    head_count = dt_bias.shape[0]
    per_group = head_count // groups
    head_size = group_width // per_group
    state_size = (conv_b.shape[1] - group_width) // 2
    gathered = lax.all_gather(tokens, "head", axis=1, tiled=True)
    normed = normalize(gathered.astype(jnp.float32), norm_gain).astype(jnp.bfloat16)
    before = from_behind(normed[local_rows - kernel_len + 1 :], SEQ, 1)
    source = jnp.concatenate([before, normed], axis=0)
    span_rows = source.shape[0]
    flat_in = w_in.reshape(w_in.shape[0], groups * w_in.shape[2])
    pieces = sent_together((flat_in, w_dt), SEQ, 0, 1)
    proj_sum = jnp.dot(source, pieces[0], preferred_element_type=jnp.float32)
    step_sum = jnp.dot(source, pieces[1], preferred_element_type=jnp.float32)
    projected = proj_sum.astype(jnp.bfloat16).reshape(span_rows, groups, w_in.shape[2])
    step_size = jax.nn.softplus(step_sum[span_rows - local_rows :] + dt_bias[None, :])
    gate_raw = projected[span_rows - local_rows :, :, :group_width]
    extended = projected[:, :, group_width:]
    summed = conv_b[None, :, :]
    for offset in range(kernel_len):
        summed = summed + conv_w[offset][None, :, :] * extended[
            offset : offset + local_rows
        ].astype(jnp.float32)
    narrow = lax.optimization_barrier(jax.nn.silu(summed).astype(jnp.bfloat16))
    convolved = narrow.astype(jnp.float32)
    inputs = convolved[:, :, :group_width].reshape(local_rows, groups, per_group, head_size)
    in_map = narrow[:, :, group_width : group_width + state_size]
    out_map = narrow[:, :, group_width + state_size :]
    step_grouped = step_size.reshape(local_rows, groups, per_group)
    log_decay = -jnp.exp(a_log).reshape(groups, per_group)[None, :, :] * step_grouped
    run_block = jax.vmap(
        partial(state_block, block_len=STRETCH), in_axes=(1, 1, 1, 1, 1), out_axes=(1, 0)
    )
    local_out, ending = run_block(inputs, step_grouped, log_decay, in_map, out_map)
    totals = jnp.sum(log_decay, axis=0)
    identity = (jnp.zeros_like(totals), jnp.zeros_like(ending))
    prior_decay, incoming = entering((totals, ending), SEQ, link_states, identity)
    cumulative = jnp.exp(jnp.cumsum(log_decay, axis=0))
    carried = (
        jnp.einsum("tgn,ghpn->tghp", out_map.astype(jnp.float32), incoming, precision=HIGHEST)
        * cumulative[:, :, :, None]
    )
    outputs = local_out + carried + d_skip.reshape(groups, per_group)[None, :, :, None] * inputs
    gated = outputs.reshape(local_rows, groups, group_width) * jax.nn.silu(
        gate_raw.astype(jnp.float32)
    )
    normed_out = normalize(gated, gate_gain[None, :, :]).astype(jnp.bfloat16)
    flat_out = normed_out.reshape(local_rows, groups * group_width)
    terms = jnp.dot(
        flat_out,
        w_out.reshape(groups * group_width, w_out.shape[2]),
        preferred_element_type=jnp.float32,
    )
    return lax.psum_scatter(terms.astype(jnp.bfloat16), "head", scatter_dimension=1, tiled=True)


def solution(mesh):
    split = Mesh(mesh.devices.reshape(4, 8, mesh.shape["head"]), ("seq_0", "seq_1", "head"))
    in_specs = (
        P(SEQ, "head"),
        P(),
        P(SEQ, "head", None),
        P(SEQ, "head"),
        P("head"),
        P("head"),
        P("head"),
        P(None, "head", None),
        P("head", None),
        P("head", None),
        P("head", None, None),
    )
    out_specs = P(SEQ, "head")
    return jax.shard_map(body, mesh=split, in_specs=in_specs, out_specs=out_specs, check_vma=False)
```

profile of v0, /device:TPU:24, one launch (start us, length us, event | category | flops | bytes accessed | tf_op | source)
XLA Modules:
  0.0 412.8 jit_solution(1749421173129096668)
XLA Ops:
  6.5 0.7 all-gather.7.cloned.1.call-update
  7.3 0.8 copy.51
  8.1 2.0 pad_maximum_fusion
  10.2 31.9 %all-gather.7.cloned.1.call-done = bf16[384,4096]{1,0:T(8,128)(2,1)} async-done(((bf16[384,512]{1,0:T(8,128)(2,1)}), bf16[384,4096]{1,0:T(8,128)(2,1)}) %all-gather.7.cloned.1.call-update) | async-done | bytes 3145744 | tf_op jit(solution)/shard_map/all_gather | solution.py:116
  42.1 2.7 fusion.45
  44.9 0.1 copy-done
  45.0 1.1 fusion.47
  46.1 3.5 collective-permute-start
  49.7 4.3 %collective-permute-done = bf16[3,4096]{1,0:T(4,128)(2,1)S(1)} collective-permute-done((bf16[3,4096]{1,0:T(4,128)(2,1)S(1)}, bf16[3,4096]{1,0:T(4,128)(2,1)S(1)}, u32[]{:S(2)}, u32[]{:S(2)}) %collective-permute-start) | collective-permute-done | bytes 24608 | tf_op jit(solution)/shard_map/ppermute | solution.py:20
  54.0 144.4 %all-gather.9.cloned.1.call-done = bf16[4096,2320]{1,0:T(8,128)(2,1)} async-done(((bf16[128,2320]{1,0:T(8,128)(2,1)}), bf16[4096,2320]{1,0:T(8,128)(2,1)}) %all-gather.9.cloned.1.call-update) | async-done | bytes 19005456 | tf_op jit(solution)/shard_map/all_gather | solution.py:25
  198.4 13.4 %fusion.54 = bf16[387,1,2304]{2,0,1:T(8,128)(2,1)S(1)} fusion(bf16[4096,2320]{1,0:T(8,128)(2,1)} %all-gather.9.cloned.1.call-done, bf16[384,4096]{1,0:T(8,128)(2,1)} %copy-done.4, bf16[3,4096]{1,0:T(4,128)(2,1)S(1)} %collective-permute-done), kind=kOutput, calls=%fused_computation.61 | convolution fusion | flops 7311612928 | bytes 23827968 | tf_op jit(solution)/shard_map/dot_general | solution.py:123
  211.8 1.3 multiply_convert_fusion
  213.1 0.2 slice_convert_fusion
  213.3 1.3 copy-done.5
  214.7 2.3 fusion.162
  217.0 0.1 copy.64
  217.1 0.1 copy.65
  217.2 2.1 reshape.698
  219.3 3.2 copy.55
  222.6 59.6 %while.14 = (s32[]{:T(128)}, f32[1,16,64,128]{3,2,1,0:T(8,128)S(1)}, f32[3,1,128,16,64]{2,0,4,3,1:T(4,128)}, f32[3,1,128,16]{3,2,1,0:T(8,128)S(1)}, f32[3,1,128,...) while((s32[]{:T(128)}, ...), condition=%wide.region_3.4_spmd.clone.clone, body=%wide.region_1.3_spmd.clone.clone.sunk | while | flops 610682880 | bytes 5721559 | solution.py:100
  222.6 0.2 reduce_window_sum.44
  222.9 0.1 fusion.190
  223.1 0.1 copy.85
  223.2 0.1 copy.86
  223.3 0.4 fusion.189
  223.7 3.3 fusion.191
  227.0 1.7 fusion.188
  228.6 13.8 %dynamic_update_slice.7 = f32[3,1,128,16,64]{2,0,4,3,1:T(4,128)} dynamic-update-slice(f32[3,1,128,16,64]{2,0,4,3,1:T(4,128)} %get-tuple-element.246, f32[1,1,128,16,64]{2,0,4,3,1:T(1,128)S(1)} %bitcast.242, s32[]{:T(128)S(6)} %copy.92, s32[]{:T(128)} %constant.25.clone.1..sunk, s32[]{:T(128)} %constant.25.clone.1..sunk, s32[]{:T(128)} %constant.25.clone.1..sunk, s32[]{:T(128)} %constant.25.clone.1..sunk) | dynamic-update-slice | bytes 1048580 | tf_op jit(solution)/shard_map/vmap()/while/body/jit(dynamic_update_index_in_dim)/dynamic_update_slice | solution.py:100
  242.5 0.2 reduce_window_sum.44
  242.7 0.1 fusion.190
  243.0 0.1 copy.85
  243.1 0.1 copy.86
  243.1 0.4 fusion.189
  243.6 3.3 fusion.191
  246.8 1.7 fusion.188
  248.5 13.8 %dynamic_update_slice.7 = f32[3,1,128,16,64]{2,0,4,3,1:T(4,128)} dynamic-update-slice(f32[3,1,128,16,64]{2,0,4,3,1:T(4,128)} %get-tuple-element.246, f32[1,1,128,16,64]{2,0,4,3,1:T(1,128)S(1)} %bitcast.242, s32[]{:T(128)S(6)} %copy.92, s32[]{:T(128)} %constant.25.clone.1..sunk, s32[]{:T(128)} %constant.25.clone.1..sunk, s32[]{:T(128)} %constant.25.clone.1..sunk, s32[]{:T(128)} %constant.25.clone.1..sunk) | dynamic-update-slice | bytes 1048580 | tf_op jit(solution)/shard_map/vmap()/while/body/jit(dynamic_update_index_in_dim)/dynamic_update_slice | solution.py:100
  262.4 0.2 reduce_window_sum.44
  262.6 0.1 fusion.190
  262.9 0.1 copy.86
  263.0 0.4 fusion.189
  263.4 3.3 fusion.191
  266.7 1.7 fusion.188
  268.4 13.8 %dynamic_update_slice.7 = f32[3,1,128,16,64]{2,0,4,3,1:T(4,128)} dynamic-update-slice(f32[3,1,128,16,64]{2,0,4,3,1:T(4,128)} %get-tuple-element.246, f32[1,1,128,16,64]{2,0,4,3,1:T(1,128)S(1)} %bitcast.242, s32[]{:T(128)S(6)} %copy.92, s32[]{:T(128)} %constant.25.clone.1..sunk, s32[]{:T(128)} %constant.25.clone.1..sunk, s32[]{:T(128)} %constant.25.clone.1..sunk, s32[]{:T(128)} %constant.25.clone.1..sunk) | dynamic-update-slice | bytes 1048580 | tf_op jit(solution)/shard_map/vmap()/while/body/jit(dynamic_update_index_in_dim)/dynamic_update_slice | solution.py:100
  282.2 0.7 convert_element_type.382
  283.1 0.6 dynamic-slice
  284.3 0.2 dynamic-update-slice
  284.5 15.6 %all-reduce = bf16[128]{0:T(256)(128)(2,1)S(1)} all-reduce(bf16[128]{0:T(256)(128)(2,1)S(1)} %dynamic-update-slice), channel_id=2, replica_groups=mesh['seq_0'=4,'seq_1'=8,'head'=8] {'seq_1'}, use_global_device_ids=true, to_apply=%add | all-reduce | flops 128 | bytes 512
  300.1 0.1 fusion.156
  300.2 0.1 convert_exponential_fusion.6
  300.3 22.5 %all-gather.13.cloned.1.call-done = bf16[8,16,64,128]{3,2,1,0:T(8,128)(2,1)} async-done(((bf16[1,16,64,128]{3,2,1,0:T(8,128)(2,1)}), bf16[8,16,64,128]{3,2,1,0:T(8,128)(2,1)}) %all-gather.13.cloned.1.call-update) | async-done | bytes 2097168 | tf_op jit(solution)/shard_map/all_gather | solution.py:44
  322.8 2.8 fusion.106
  325.7 7.0 %all_gather.27 = bf16[4,1,16]{2,1,0:T(2,128)(2,1)S(1)} all-gather(bf16[1,1,16]{2,1,0:T(2,128)(2,1)S(1)} %get-tuple-element.156), channel_id=1, replica_groups=mesh['seq_0'=4,'seq_1'=8,'head'=8] {'seq_0'}, dimensions={0}, use_global_device_ids=true | all-gather | bytes 160 | tf_op jit(solution)/shard_map/all_gather | solution.py:44
  332.7 0.5 copy.62
  333.1 0.9 reduce-window.6
  334.0 0.2 slice_reduce_fusion
  334.2 0.1 copy.68
  334.3 0.1 broadcast.322
  334.4 2.8 transpose.64
  337.2 12.7 %all-gather.11.cloned.1.call-done = bf16[4,1,16,64,128]{4,3,2,1,0:T(8,128)(2,1)} async-done(((bf16[1,1,16,64,128]{4,3,2,1,0:T(8,128)(2,1)}), bf16[4,1,16,64,128]{4,3,2,1,0:T(8,128)(2,1)}) %all-gather.11.cloned.1.call-update) | async-done | bytes 1048592 | tf_op jit(solution)/shard_map/all_gather | solution.py:44
  350.0 4.7 %fusion.69 = f32[384,1,16,64]{0,3,2,1:T(8,128)} fusion(f32[384,1,16,64]{0,3,2,1:T(8,128)S(1)} %transpose.64, f32[384,1,16,64]{0,3,2,1:T(8,128)S(1)} %bitcast.245, f32[16]{0:T(128)S(1)} %copy-done.12, f32[384,16]{0,1:T(8,128)S(1)} %fusion.139, bf16[4,1,16,64,128]{4,3,2,1,0:T(8,128)(2,1)} %all-gather.11.cloned.1.call-done, f32[16]{0:T(128)S(1)} %get-tuple-element.173, ...), kind=kOutput, calls=%fused_computation.78 | convolution fusion | flops 611844096 | bytes 7988108 | tf_op jit(solution)/shard_map/tgn,ghpn->tghp/dot_general | solution.py:150
  354.7 2.0 copy.63
  356.7 0.7 multiply_reduce_fusion
  357.4 8.7 %fusion.48 = bf16[384,4096]{1,0:T(8,128)(2,1)} fusion(bf16[1,1024,4096]{2,1,0:T(8,128)(2,1)} %param.23, f32[1024]{0:T(1024)S(1)} %bitcast.251, f32[384]{0:T(512)S(1)} %add_rsqrt_fusion, f32[384,1,1024]{2,0,1:T(8,128)S(1)} %copy.63, bf16[387,1,2304]{2,0,1:T(8,128)(2,1)S(1)} %copy-done.2), kind=kOutput, calls=%fused_computation.59 | convolution fusion | flops 3226337280 | bytes 13899776 | tf_op jit(solution)/shard_map/dot_general | solution.py:159
  366.1 40.2 %reduce-scatter.2.cloned.1.call-done = bf16[384,512]{1,0:T(8,128)(2,1)} async-done(((bf16[384,4096]{1,0:T(8,128)(2,1)}), bf16[384,512]{1,0:T(8,128)(2,1)}) %reduce-scatter.2.cloned.1.call-update) | async-done | bytes 393232 | tf_op jit(solution)/shard_map/reduce_scatter | solution.py:164
  (74 shorter events, 1.2 us)
Async XLA Ops:
  6.5 3.6 copy-start.10
  6.5 35.6 %all-gather.7.cloned.1.call-start = ((), (), s32[]{:S(2)}) async-start(), calls=%async_computation.1 | async-start | bytes 3538944 | tf_op jit(solution)/shard_map/all_gather | solution.py:116
  7.3 191.1 %all-gather.9.cloned.1.call-start = ((), (), s32[]{:S(2)}) async-start(), calls=%async_computation.2 | async-start | bytes 20545536 | tf_op jit(solution)/shard_map/all_gather | solution.py:25
  10.1 34.8 %copy-start.7 = (f32[4096]{0:T(1024)S(1)}, f32[4096]{0:T(1024)}, u32[]{:S(2)}) copy-start(f32[4096]{0:T(1024)} %param.14) | copy-start | bytes 49156
  10.1 312.7 %all-gather.13.cloned.1.call-start = ((), (), s32[]{:S(2)}) async-start(), calls=%async_computation.5 | async-start | bytes 2359296 | tf_op jit(solution)/shard_map/all_gather | solution.py:44
  42.1 2.8 copy-start
  45.0 4.6 %copy-start.6 = (f32[4,1,1280]{2,1,0:T(1,128)S(1)}, f32[4,1,1280]{2,1,0:T(1,128)}, u32[]{:S(2)}) copy-start(f32[4,1,1280]{2,1,0:T(1,128)} %param.20) | copy-start | bytes 61444
  45.0 4.7 %copy-start.8 = (f32[1,1280]{1,0:T(1,128)S(1)}, f32[1,1280]{1,0:T(1,128)}, u32[]{:S(2)}) copy-start(f32[1,1280]{1,0:T(1,128)} %param.21) | copy-start | bytes 15364
  46.1 3.5 copy-start.4
  46.1 7.9 %collective-permute-start = (bf16[3,4096]{1,0:T(4,128)(2,1)S(1)}, bf16[3,4096]{1,0:T(4,128)(2,1)S(1)}, u32[]{:S(2)}, u32[]{:S(2)}) collective-permute-start(bf16[3,4096]{1,0:T(4,128)(2,1)S(1)} %slice.201), channel_id=1, source_target_pairs={{0,8},{8,16},{16,24},{24,32},{32,40},{40,48},{48,56},{56,64},{64,7... | collective-permute-start | bytes 73736 | tf_op jit(solution)/shard_map/ppermute | solution.py:20
  211.7 1.3 copy-start.1
  211.7 2.9 copy-start.5
  213.1 3.9 copy-start.3
  213.1 1.5 copy-start.11
  222.6 60.5 %copy-start.13 = (u32[256]{0:T(256)S(1)}, u32[256]{0:T(256)}, u32[]{:S(2)}) copy-start(u32[256]{0:T(256)} %constant.77) | copy-start | bytes 3076
  283.0 67.0 %all-gather.11.cloned.1.call-start = ((), (), s32[]{:S(2)}) async-start(), calls=%async_computation.3 | async-start | bytes 1310720 | tf_op jit(solution)/shard_map/all_gather | solution.py:44
  325.6 80.7 %reduce-scatter.2.cloned.1.call-start = ((), (), s32[]{:S(2)}) async-start(), calls=%async_computation.4 | async-start | bytes 3538944 | tf_op jit(solution)/shard_map/reduce_scatter | solution.py:164
  334.0 16.0 %copy-start.12 = (f32[16]{0:T(128)S(1)}, f32[16]{0:T(128)}, u32[]{:S(2)}) copy-start(f32[16]{0:T(128)} %param.19) | copy-start | bytes 196
  354.7 2.0 copy-start.2
  356.7 0.7 copy-start.9
Sparse Core Ops, SparseCore 0:
  9.2 32.9 all-gather.6
  44.7 153.6 all-gather.8
  283.1 39.6 all-gather.12
  325.7 24.1 all-gather.10
  366.2 40.0 reduce-scatter.1
where the time goes:
time: 415 us; the launch traced here: 413 us
  waiting for transfers between devices  257 us (62%)
  local copies, waits for them, and re-layouts  56.7 us (14%)
  matrix products  45.5 us (11%)
  blocking collectives  22.6 us (5%)
  between operations  14.1 us (3%)
  other arithmetic  13.3 us (3%)
    all_gather x1, waiting for transfers between devices, sent_together(): lax.all_gather(both, axis, axis=dim, tiled=True)  144 us
    dynamic_update_slice x3, local copies, waits for them, and re-layouts, state_block(): final, outputs = lax.scan(advance, start_state, shaped)  41.5 us
    reduce_scatter x1, waiting for transfers between devices, body(): lax.psum_scatter(terms.astype(jnp.bfloat16), 'head', scatter_dimension=1,...  40.2 us
    all_gather x2, waiting for transfers between devices, entering(): lax.all_gather(part.astype(kind), axis)  35.3 us
    all_gather x1, waiting for transfers between devices, body(): gathered = lax.all_gather(tokens, 'head', axis=1, tiled=True)  31.9 us
    unnamed x1, blocking collectives  15.6 us
    dot_general x1, matrix products, body(): proj_sum = jnp.dot(source, pieces[0], preferred_element_type=jnp.float32)  13.4 us
    dot_general x3, matrix products, advance(): within = jnp.einsum('ijh,jhp->ihp', weights, stretch_in, precision=HIGHEST)  9.81 us
  transfers between devices with their start and end apart: 6, of which 6 were waited for; matrix products, arithmetic and copies ran while one was open for 3% of the time, Pallas kernels for 0%

commit v1 on v0

v1 whole, which is shorter than its diff:
```python
import heapq
import itertools

import jax
import jax.numpy as jnp
from jax import lax
from jax.experimental import pallas as pl
from jax.experimental.pallas import tpu as pltpu
from jax.sharding import PartitionSpec as P

EPS = 1e-05
HIGHEST = lax.Precision.HIGHEST
MESH = pl.DeviceIdType.MESH
F32 = jnp.float32
BF16 = jnp.bfloat16

NY, NZ, NX = 4, 8, 4
ROWS = 384
DB = 512
HB = 8
SUB = 128
CC = 1280
GC = 1024
YZ_ROWS = 48
NH = 16
CHUNKS = 3


def children(stream, dy, dz):
    along_z, flip = stream in (0, 2), stream >= 2
    out = []
    if along_z:
        up, down = (3, 4) if flip else (4, 3)
        if dy == 0:
            if 0 <= dz < up:
                out.append((0, dz + 1, "z+"))
            if 0 <= -dz < down:
                out.append((0, dz - 1, "z-"))
            out.append((1, dz, "y+"))
            out.append((-1, dz, "y-"))
        far = 1 if (dz % 2 == 0) != flip else -1
        if dy == far:
            out.append((2 * far, dz, "y+" if far > 0 else "y-"))
    else:
        far = -1 if flip else 1
        if dz == 0:
            if dy == 0:
                out += [(1, 0, "y+"), (-1, 0, "y-")]
            if dy == far:
                out.append((2 * far, 0, "y+" if far > 0 else "y-"))
        up, down = (4, 3) if (dy % 2 == 0) != flip else (3, 4)
        if 0 <= dz < up:
            out.append((dy, dz + 1, "z+"))
        if 0 <= -dz < down:
            out.append((dy, dz - 1, "z-"))
    return out


def arrival_order(late):
    sizes = [(SUB - YZ_ROWS) * CC, YZ_ROWS * CC, (SUB - YZ_ROWS) * GC, YZ_ROWS * GC]
    free = {d: 0.0 for d in ("y+", "y-", "z+", "z-")}
    events, order, tick = [], [], itertools.count()

    def issue(t, stream, dy, dz):
        for a, b, d in children(stream, dy, dz):
            end = max(t, free[d]) + sizes[stream] / 21600.0
            free[d] = end
            heapq.heappush(events, (end + 2.0, next(tick), stream, a, b))

    issue(0.0, 0, 0, 0)
    issue(0.0, 1, 0, 0)
    while events:
        t, _, stream, a, b = heapq.heappop(events)
        order.append((stream, a, b))
        issue(t, stream, a, b)
        if len(order) == late:
            issue(t, 2, 0, 0)
            issue(t, 3, 0, 0)
    return order


LATE = 54
ORDER = arrival_order(LATE)
LAST_C = max(i for i, item in enumerate(ORDER) if item[0] < 2) + 1


def number(dy, dz):
    return (dy % NY) * NZ + dz % NZ


def softplus(v):
    return jnp.maximum(v, 0.0) + jnp.log1p(jnp.exp(-jnp.abs(v)))


def silu(v):
    return v / (1.0 + jnp.exp(-v))


def dot_nt(a, b):
    return lax.dot_general(a, b, (((1,), (1,)), ((), ())), preferred_element_type=F32)


def dot_tn(a, b):
    return lax.dot_general(a, b, (((0,), (0,)), ((), ())), preferred_element_type=F32)


def kernel(
    tok_in, w_in, w_dt, w_out, norm_gain, dt_bias, a_log, d_skip, conv_w, conv_b, gate_gain,
    out_ref,
    tok, xn, wc, wg, wd, wo, chf, halo_out, halo_in, cv, ybuf, tt, ct, fs,
    e_out, d_out, e_in, d_in, pre, row_out, rowd_out, row_in, rowd_in, back_out, sin,
    no, sib_out, sib_in, part, far_out, far_in, near_out, near_in,
    load_sem, w_send, w_recv, t_send, t_recv, h_send, h_recv,
    s_send, s_recv, r_send, r_recv, b_send, b_recv, o_send, o_recv, x_send, x_recv,
):
    s = lax.axis_index("seq")
    hd = lax.axis_index("head")
    y, z = lax.div(s, NZ), lax.rem(s, NZ)
    x, c = lax.div(hd, 2), lax.rem(hd, 2)

    def at_yz(dy, dz):
        return lax.rem(y + dy + 2 * NY, NY) * NZ + lax.rem(z + dz + 2 * NZ, NZ)

    def head_of(dx, core):
        return lax.rem(x + dx + NX, NX) * 2 + core

    sibling = (s, x * 2 + (1 - c))
    plus, minus = (s, head_of(1, c)), (s, head_of(-1, c))
    follow = (lax.rem(s + 1, NY * NZ), hd)
    ahead = (lax.rem(s + NY * NZ - 1, NY * NZ), hd)
    target = {
        "y+": (at_yz(1, 0), hd), "y-": (at_yz(-1, 0), hd),
        "z+": (at_yz(0, 1), hd), "z-": (at_yz(0, -1), hd),
    }
    z_peers = [(at_yz(0, k), hd) for k in range(1, NZ)]
    y_peers = [(at_yz(k, 0), hd) for k in range(1, NY)]
    sent = []

    def remote(src, dst, send, recv, where):
        return pltpu.make_async_remote_copy(
            src_ref=src, dst_ref=dst, send_sem=send, recv_sem=recv, device_id=where, device_id_type=MESH
        )

    def push(src, dst, send, recv, where):
        copy = remote(src, dst, send, recv, where)
        copy.start()
        sent.append(copy)

    def arrived(ref, recv):
        remote(ref, ref, recv, recv, sibling).wait_recv()

    own_rows = pl.ds(pl.multiple_of(s * SUB, SUB), SUB)
    loads = [
        pltpu.make_async_copy(tok_in, tok.at[hd], load_sem.at[0]),
        pltpu.make_async_copy(w_in.at[:, pl.ds(GC, CC)], wc.at[own_rows, :], load_sem.at[1]),
        pltpu.make_async_copy(w_dt, wd.at[:, own_rows], load_sem.at[2]),
        pltpu.make_async_copy(w_in.at[:, pl.ds(0, GC)], wg.at[own_rows, :], load_sem.at[3]),
        pltpu.make_async_copy(w_out, wo, load_sem.at[4]),
    ]
    for copy in loads:
        copy.start()

    barrier = pltpu.get_barrier_semaphore()
    peers = z_peers + y_peers + [plus, minus, sibling, follow, ahead]
    for peer in peers:
        pl.semaphore_signal(barrier, inc=1, device_id=peer, device_id_type=MESH)
    pl.semaphore_wait(barrier, len(peers))

    def block(stream, slot):
        base = slot * SUB
        held = wc if stream < 2 else wg
        if stream in (0, 2):
            return held.at[pl.ds(pl.multiple_of(base + YZ_ROWS, 16), SUB - YZ_ROWS), :]
        return held.at[pl.ds(pl.multiple_of(base, 16), YZ_ROWS), :]

    def dt_block(slot):
        return wd.at[:, pl.ds(pl.multiple_of(slot * SUB, SUB), SUB)]

    def spread(stream, dy, dz):
        slot = at_yz(-dy, -dz)
        for a, b, d in children(stream, dy, dz):
            k = number(a, b)
            piece = block(stream, slot)
            push(piece, piece, w_send.at[stream, k], w_recv.at[stream, k], target[d])
            if stream == 0:
                piece = dt_block(slot)
                push(piece, piece, w_send.at[4, k], w_recv.at[4, k], target[d])

    state = {"at": 0}

    def pump(count, stop=len(ORDER)):
        for _ in range(count):
            if state["at"] >= stop:
                return
            stream, dy, dz = ORDER[state["at"]]
            state["at"] += 1
            slot, k = at_yz(-dy, -dz), number(dy, dz)
            arrived(block(stream, slot), w_recv.at[stream, k])
            if stream == 0:
                arrived(dt_block(slot), w_recv.at[4, k])
            spread(stream, dy, dz)
            if state["at"] == LATE:
                spread(2, 0, 0)
                spread(3, 0, 0)

    loads[1].wait()
    loads[2].wait()
    spread(0, 0, 0)
    spread(1, 0, 0)
    loads[0].wait()

    half = [pl.ds(0, ROWS // 2), pl.ds(ROWS // 2, ROWS // 2)]

    def tok_piece(dx, core, k):
        return tok.at[head_of(dx, core), half[k], :]

    mine = [tok_piece(0, c, 0), tok_piece(0, c, 1)]
    push(mine[0], mine[0], t_send.at[0], t_recv.at[0], plus)
    push(mine[1], mine[1], t_send.at[3], t_recv.at[3], minus)
    push(mine[1], mine[1], t_send.at[1], t_recv.at[1], plus)
    push(mine[0], mine[0], t_send.at[2], t_recv.at[2], minus)
    push(tok.at[hd], tok.at[hd], t_send.at[6], t_recv.at[6], sibling)

    def relay(index, dx, k, twin, onward=None, onward_index=None):
        piece = tok_piece(dx, c, k)
        arrived(piece, t_recv.at[index])
        if onward is not None:
            push(piece, piece, t_send.at[onward_index], t_recv.at[onward_index], onward)
        push(piece, piece, t_send.at[twin], t_recv.at[twin], sibling)

    loads[3].wait()
    pump(4)
    relay(0, -1, 0, 7, plus, 4)
    relay(3, 1, 1, 10, minus, 5)
    pump(5)
    relay(1, -1, 1, 8)
    relay(2, 1, 0, 9)
    pump(5)
    relay(4, 2, 0, 11)
    relay(5, 2, 1, 12)
    pump(2)
    arrived(tok.at[head_of(0, 1 - c)], t_recv.at[6])
    for index, dx, k in ((7, -1, 0), (8, -1, 1), (9, 1, 0), (10, 1, 1), (11, 2, 0), (12, 2, 1)):
        arrived(tok_piece(dx, 1 - c, k), t_recv.at[index])

    def norm_rows(i, carry):
        rows = pl.ds(pl.multiple_of(i * 32, 32), 32)
        total = jnp.zeros((32, 1), F32)
        for h in range(HB):
            v = tok[h, rows, :].astype(F32)
            total = total + jnp.sum(v * v, axis=1, keepdims=True)
        scale = lax.rsqrt(total / (HB * DB) + EPS)
        for h in range(HB):
            v = tok[h, rows, :].astype(F32)
            xn[h, rows, :] = (v * scale * norm_gain[:, h * DB : (h + 1) * DB]).astype(BF16)
        return carry

    for part_of in range(4):
        lax.fori_loop(part_of * 3, part_of * 3 + 3, norm_rows, 0)
        pump(1)
    pump(len(ORDER), LAST_C)

    def channel_tile(i, carry):
        cols = pl.ds(pl.multiple_of(i * 256, 256), 256)
        total = jnp.zeros((ROWS, 256), F32)
        for h in range(HB):
            total = total + jnp.dot(xn[h], wc[h * DB : (h + 1) * DB, cols], preferred_element_type=F32)
        rounded = total.astype(BF16)
        halo_out[:, cols] = rounded[ROWS - 16 :, :]
        chf[8:, cols] = rounded.astype(F32)
        return carry

    for tile in range(5):
        lax.fori_loop(tile, tile + 1, channel_tile, 0)
        pump(1)

    raw = jnp.zeros((NH, ROWS), F32)
    for h in range(HB):
        raw = raw + dot_nt(wd[:, h * DB : (h + 1) * DB], xn[h])

    def column_of(ref):
        wide = jnp.concatenate([ref[...], jnp.zeros((1, 128 - NH), F32)], axis=1)
        return jnp.transpose(jnp.broadcast_to(wide, (128, 128)))[:NH, :1]

    push(halo_out, halo_in, h_send, h_recv, follow)
    step = softplus(raw + column_of(dt_bias))
    decay = -jnp.exp(column_of(a_log)) * step
    row_id = lax.broadcasted_iota(jnp.int32, (128, 128), 0)
    lane_id = lax.broadcasted_iota(jnp.int32, (128, 128), 1)
    upper = jnp.where(row_id <= lane_id, 1.0, 0.0).astype(F32)
    first_half = lane_id < 64
    upper_rows = row_id < 64
    for q in range(CHUNKS):
        span = slice(q * 128, (q + 1) * 128)
        cum = jnp.dot(decay[:, span], upper, precision=HIGHEST, preferred_element_type=F32)
        to_end = jnp.exp(cum[:, 127:128] - cum) * step[:, span]
        ct[q] = cum
        stacked = jnp.concatenate(
            [cum, to_end, step[:, span], jnp.exp(cum), jnp.zeros((64, 128), F32)], axis=0
        )
        tt[q] = jnp.transpose(stacked)
    pump(2)

    arrived(halo_in, h_recv)
    chf[:8, :] = jnp.where(s > 0, halo_in[8:16, :].astype(F32), 0.0)

    def conv_tile(i, carry):
        cols = pl.ds(pl.multiple_of(i * 128, 128), 128)
        for q in range(CHUNKS):
            total = conv_b[:, cols] + jnp.zeros((128, 128), F32)
            for k in range(4):
                total = total + conv_w[k : k + 1, cols] * chf[q * 128 + 5 + k : q * 128 + 133 + k, cols]
            cv[q * 128 : (q + 1) * 128, cols] = silu(total).astype(BF16)
        return carry

    lax.fori_loop(0, 5, conv_tile, 0)
    pump(1)
    lax.fori_loop(5, 10, conv_tile, 0)
    pump(1)

    def pair_cols(table, base, j):
        return jnp.where(
            first_half, table[:, base + 2 * j : base + 2 * j + 1], table[:, base + 2 * j + 1 : base + 2 * j + 2]
        )

    def pair_rows(row, j):
        return jnp.where(upper_rows, jnp.exp(row[:, 2 * j : 2 * j + 1]), jnp.exp(row[:, 2 * j + 1 : 2 * j + 2]))

    for q in range(CHUNKS):
        span = slice(q * 128, (q + 1) * 128)
        b_map, c_map = cv[span, 1024:1152], cv[span, 1152:1280]
        scores = jnp.where(row_id >= lane_id, dot_nt(c_map, b_map), 0.0)
        table = tt[q]
        for j in range(8):
            cols = slice(j * 128, (j + 1) * 128)
            v = cv[span, cols].astype(F32)
            stepped = v * pair_cols(table, 32, j)
            values = jnp.concatenate(
                [jnp.where(first_half, stepped, 0.0), jnp.where(first_half, 0.0, stepped)], axis=0
            ).astype(BF16)
            weights = []
            for h in (2 * j, 2 * j + 1):
                gap = jnp.minimum(table[:, h : h + 1] - ct[q, h : h + 1, :], 0.0)
                weights.append((scores * jnp.exp(gap)).astype(BF16))
            inner = jnp.dot(jnp.concatenate(weights, axis=1), values, preferred_element_type=F32)
            skip = jnp.where(first_half[:1], d_skip[:, 2 * j : 2 * j + 1], d_skip[:, 2 * j + 1 : 2 * j + 2])
            ybuf[span, cols] = inner + skip * v
            fs[q, cols, :] = dot_tn((v * pair_cols(table, 16, j)).astype(BF16), b_map)
            if j % 2 == 1:
                pump(1)

    ends = [tt[q, 127:128, :] for q in range(CHUNKS)]
    for j in range(8):
        cols = slice(j * 128, (j + 1) * 128)
        total = fs[1, cols, :] + pair_rows(ends[1], j) * fs[0, cols, :]
        total = fs[2, cols, :] + pair_rows(ends[2], j) * total
        e_out[j] = total.astype(BF16)
    d_out[...] = jnp.broadcast_to(ends[0] + ends[1] + ends[2], (8, 128))
    pump(1)
    for k in range(1, NZ):
        peer = lax.rem(z + k, NZ)
        push(e_out.at[peer], e_in.at[z], s_send.at[0, k], s_recv.at[0, k], z_peers[k - 1])
        push(d_out, d_in.at[z], s_send.at[1, k], s_recv.at[1, k], z_peers[k - 1])
    e_in[z] = e_out[z]
    d_in[z] = d_out[...]
    pump(5)
    for k in range(1, NZ):
        source = lax.rem(z + NZ - k, NZ)
        arrived(e_in.at[source], s_recv.at[0, k])
        arrived(d_in.at[source], s_recv.at[1, k])

    lane_row = lax.broadcasted_iota(jnp.int32, (1, 128), 1)

    def pick(row, lane):
        return jnp.sum(jnp.where(lane_row == lane, row, 0.0), axis=1, keepdims=True)

    def factor(pair):
        return jnp.where(upper_rows[:, :1], jnp.exp(pair[0]), jnp.exp(pair[1]))

    running = jnp.zeros((128, 128), F32)
    gone = (jnp.zeros((1, 1), F32), jnp.zeros((1, 1), F32))
    before = []
    for k in range(NZ):
        pre[k] = running
        before.append(gone)
        here = d_in[k, :1, :]
        pair = (pick(here, 2 * z), pick(here, 2 * z + 1))
        running = factor(pair) * running + e_in[k].astype(F32)
        gone = (gone[0] + pair[0], gone[1] + pair[1])
    row_out[...] = running.astype(BF16)
    rowd_out[...] = jnp.broadcast_to(jnp.where(lane_row == 0, gone[0], gone[1]), (8, 128))
    pump(1)
    for k in range(1, NY):
        push(row_out, row_in.at[y], r_send.at[0, k], r_recv.at[0, k], y_peers[k - 1])
        push(rowd_out, rowd_in.at[y], r_send.at[1, k], r_recv.at[1, k], y_peers[k - 1])
    row_in[y] = row_out[...]
    rowd_in[y] = rowd_out[...]
    pump(5)
    for k in range(1, NY):
        source = lax.rem(y + NY - k, NY)
        arrived(row_in.at[source], r_recv.at[0, k])
        arrived(rowd_in.at[source], r_recv.at[1, k])
    entering = jnp.zeros((128, 128), F32)
    for k in range(NY):
        here = rowd_in[k, :1, :]
        moved = factor((here[:, 0:1], here[:, 1:2])) * entering + row_in[k].astype(F32)
        entering = jnp.where(k < y, moved, entering)
    for k in range(NZ):
        back_out[k] = (factor(before[k]) * entering + pre[k]).astype(BF16)
    pump(1)
    for k in range(1, NZ):
        peer = lax.rem(z + k, NZ)
        push(back_out.at[peer], sin.at[z], b_send.at[k], b_recv.at[k], z_peers[k - 1])
    sin[z] = back_out[z]
    pump(6)
    for k in range(1, NZ):
        arrived(sin.at[lax.rem(z + NZ - k, NZ)], b_recv.at[k])

    for j in range(8):
        cols = slice(j * 128, (j + 1) * 128)
        held = sin[j].astype(F32)
        for q in range(CHUNKS):
            span = slice(q * 128, (q + 1) * 128)
            across = dot_nt(cv[span, 1152:1280], held.astype(BF16))
            ybuf[span, cols] += pair_cols(tt[q], 48, j) * across
            if q < CHUNKS - 1:
                held = pair_rows(ends[q], j) * held + fs[q, cols, :]
        pump(1)
    pump(len(ORDER))

    def gate_tile(i, total):
        cols = pl.ds(pl.multiple_of(i * 256, 256), 256)
        raw_gate = jnp.zeros((ROWS, 256), F32)
        for h in range(HB):
            raw_gate = raw_gate + jnp.dot(xn[h], wg[h * DB : (h + 1) * DB, cols], preferred_element_type=F32)
        gated = ybuf[:, cols] * silu(raw_gate.astype(BF16).astype(F32))
        ybuf[:, cols] = gated
        return total + jnp.sum(gated * gated, axis=1, keepdims=True)

    total = lax.fori_loop(0, 4, gate_tile, jnp.zeros((ROWS, 1), F32))
    scale = lax.rsqrt(total / GC + EPS)

    def norm_tile(i, carry):
        cols = pl.ds(pl.multiple_of(i * 128, 128), 128)
        no[:, cols] = (ybuf[:, cols] * scale * gate_gain[:, cols]).astype(BF16)
        return carry

    lax.fori_loop(0, 8, norm_tile, 0)
    loads[4].wait()

    def term(dx, core):
        cols = pl.ds(pl.multiple_of(head_of(dx, core) * DB, DB), DB)
        return jnp.dot(no[...], wo[:, cols], preferred_element_type=F32)

    top, low = half
    order = (2, 1, 3, 0)
    for r in order:
        sib_out[r] = term(r, 1 - c).astype(BF16)
        push(sib_out.at[r], sib_in.at[r], o_send.at[r], o_recv.at[r], sibling)
        part[r] = term(r, c)

    def chip_sum(r, rows):
        return part[r, rows, :] + sib_in[r, rows, :].astype(F32)

    arrived(sib_in.at[2], o_recv.at[2])
    far_out[...] = chip_sum(2, slice(None)).astype(BF16)
    push(far_out.at[top, :], far_in.at[0], x_send.at[0], x_recv.at[0], plus)
    push(far_out.at[low, :], far_in.at[1], x_send.at[1], x_recv.at[1], minus)
    arrived(sib_in.at[1], o_recv.at[1])
    near_out[0, low, :] = chip_sum(1, low).astype(BF16)
    push(near_out.at[0, low, :], near_in.at[0, low, :], x_send.at[2], x_recv.at[2], plus)
    arrived(sib_in.at[3], o_recv.at[3])
    near_out[1, top, :] = chip_sum(3, top).astype(BF16)
    push(near_out.at[1, top, :], near_in.at[1, top, :], x_send.at[3], x_recv.at[3], minus)
    arrived(far_in.at[0], x_recv.at[0])
    near_out[0, top, :] = (chip_sum(1, top) + far_in[0].astype(F32)).astype(BF16)
    push(near_out.at[0, top, :], near_in.at[0, top, :], x_send.at[4], x_recv.at[4], plus)
    arrived(far_in.at[1], x_recv.at[1])
    near_out[1, low, :] = (chip_sum(3, low) + far_in[1].astype(F32)).astype(BF16)
    push(near_out.at[1, low, :], near_in.at[1, low, :], x_send.at[5], x_recv.at[5], minus)
    arrived(sib_in.at[0], o_recv.at[0])
    part[0] = chip_sum(0, slice(None))
    arrived(near_in.at[0, low, :], x_recv.at[2])
    arrived(near_in.at[1, top, :], x_recv.at[3])
    arrived(near_in.at[0, top, :], x_recv.at[4])
    arrived(near_in.at[1, low, :], x_recv.at[5])
    out_ref[...] = (part[0] + near_in[0].astype(F32) + near_in[1].astype(F32)).astype(BF16)
    for copy in sent:
        copy.wait_send()


def body(tokens, norm_gain, w_in, w_dt, dt_bias, a_log, d_skip, conv_w, conv_b, gate_gain, w_out):
    any_space = pl.BlockSpec(memory_space=pl.ANY)
    vmem = pl.BlockSpec(memory_space=pltpu.VMEM)
    dma = pltpu.SemaphoreType.DMA

    def buf(*shape, dtype=BF16):
        return pltpu.VMEM(shape, dtype)

    scratch = [
        buf(HB, ROWS, DB), buf(HB, ROWS, DB), buf(4096, CC), buf(4096, GC), buf(NH, 4096), buf(GC, 4096),
        buf(ROWS + 8, CC, dtype=F32), buf(16, CC), buf(16, CC), buf(ROWS, CC), buf(ROWS, GC, dtype=F32),
        buf(CHUNKS, 128, 128, dtype=F32), buf(CHUNKS, NH, 128, dtype=F32), buf(CHUNKS, GC, 128, dtype=F32),
        buf(8, 128, 128), buf(8, 128, dtype=F32), buf(8, 128, 128), buf(8, 8, 128, dtype=F32),
        buf(8, 128, 128, dtype=F32),
        buf(128, 128), buf(8, 128, dtype=F32), buf(NY, 128, 128), buf(NY, 8, 128, dtype=F32),
        buf(8, 128, 128), buf(8, 128, 128),
        buf(ROWS, GC), buf(4, ROWS, DB), buf(4, ROWS, DB), buf(4, ROWS, DB, dtype=F32),
        buf(ROWS, DB), buf(2, ROWS // 2, DB), buf(2, ROWS, DB), buf(2, ROWS, DB),
        dma((5,)), dma((5, 32)), dma((5, 32)), dma((13,)), dma((13,)), dma, dma,
        dma((2, NZ)), dma((2, NZ)), dma((2, NY)), dma((2, NY)), dma((NZ,)), dma((NZ,)),
        dma((4,)), dma((4,)), dma((6,)), dma((6,)),
    ]
    return pl.pallas_call(
        kernel,
        out_shape=jax.ShapeDtypeStruct((ROWS, DB), BF16),
        in_specs=[any_space] * 4 + [vmem] * 7,
        out_specs=vmem,
        scratch_shapes=scratch,
        compiler_params=pltpu.CompilerParams(
            collective_id=0, has_side_effects=True, vmem_limit_bytes=64 * 1024 * 1024 - 65536
        ),
    )(
        tokens, w_in.reshape(SUB, GC + CC), w_dt.T, w_out.reshape(GC, 4096),
        norm_gain.reshape(1, 4096), dt_bias.reshape(1, NH), a_log.reshape(1, NH), d_skip.reshape(1, NH),
        conv_w.reshape(4, CC), conv_b, gate_gain,
    )


def solution(mesh):
    in_specs = (
        P("seq", "head"), P(), P("seq", "head", None), P("seq", "head"), P("head"), P("head"), P("head"),
        P(None, "head", None), P("head", None), P("head", None), P("head", None, None),
    )
    return jax.shard_map(body, mesh=mesh, in_specs=in_specs, out_specs=P("seq", "head"), check_vma=False)
```

time: 415 us -> 162 us (0.39)
  waiting for transfers between devices: 257 us -> 0 us
  Pallas kernels: 0 us -> 158 us
  local copies, waits for them, and re-layouts: 56.7 us -> 3.11 us
  matrix products: 45.5 us -> 0 us
  blocking collectives: 22.6 us -> 0 us
  between operations: 14.1 us -> 0.01 us
  other arithmetic: 13.3 us -> 0 us
    all_gather x4 -> x0, waiting for transfers between devices: 212 us -> none  [the longest x1 144 us: sent_together(): lax.all_gather(both, axis, axis=dim, tiled=True)]
    pallas_call x0 -> x1, Pallas kernels: none -> 158 us  [body(): pl.pallas_call(kernel, out_shape=jax.ShapeDtypeStruct((ROWS, DB), BF16),...]
    dot_general x16 -> x0, matrix products: 45.5 us -> none  [the longest x1 13.4 us: body(): proj_sum = jnp.dot(source, pieces[0], preferred_element_type=jnp.float32)]
    dynamic_update_slice x3 -> x0, local copies, waits for them, and re-layouts: 41.5 us -> none  [state_block(): final, outputs = lax.scan(advance, start_state, shaped)]
    reduce_scatter x1 -> x0, waiting for transfers between devices: 40.2 us -> none  [body(): lax.psum_scatter(terms.astype(jnp.bfloat16), 'head', scatter_dimension=1,...]
    unnamed x1 -> x0, blocking collectives: 15.6 us -> none
    all_gather x1 -> x0, blocking collectives: 6.97 us -> none  [entering(): lax.all_gather(part.astype(kind), axis)]
    convert_element_type x4 -> x0, other arithmetic: 5.92 us -> none  [the longest x2 3.52 us: entering(): part.astype(kind)]
  transfers between devices with their start and end apart: 6 -> 0, of which waited for: 6 -> 0; matrix products, arithmetic and copies ran while one was open for 3% -> 0% of each run, Pallas kernels for 0% -> 0%
where the time goes in v1:
time: 162 us; the launch traced here: 161 us
  Pallas kernels  158 us (98%)
  local copies, waits for them, and re-layouts  3.11 us (2%)
    pallas_call x1, Pallas kernels, body(): pl.pallas_call(kernel, out_shape=jax.ShapeDtypeStruct((ROWS, DB), BF16),...  158 us

profile of v1, /device:TPU:24, one launch (start us, length us, event | category | flops | bytes accessed | tf_op | source)
XLA Modules:
  0.0 161.3 jit_solution(15271809956181737936)
XLA Ops:
  0.0 1.3 copy.14
  1.3 158.2 %shard_map.109 = bf16[384,512]{1,0:T(8,128)(2,1)} custom-call(bf16[384,512]{1,0:T(8,128)(2,1)} %tok_in.1, bf16[128,2304]{1,0:T(8,128)(2,1)} %bitcast.11, bf16[16,128]{1,0:T(8,128)(2,1)} %bitcast.14, bf16[1024,4096]{1,0:T(8,128)(2,1)} %bitcast.10, f32[1,4096]{1,0:T(1,128)} %bitcast.13, f32[1,16]{1,0:T(1,128)} %bitcast.15, f32[1,16]{1,0:T(1,128)} %bitcast.16, ...), custom_call_target="tpu_custom_call" | custom-call | tf_op jit(solution)/shard_map/pallas_call | solution.py:514
  159.5 1.8 %copy.16 = bf16[384,512]{1,0:T(8,128)(2,1)} copy(bf16[384,512]{1,0:T(8,128)(2,1)} %shard_map.109) | data formatting | bytes 786432

commit v2 on v1

v2 whole, which is shorter than its diff:
```python
import heapq
import itertools

import jax
import jax.numpy as jnp
from jax import lax
from jax.experimental import pallas as pl
from jax.experimental.pallas import tpu as pltpu
from jax.sharding import PartitionSpec as P

EPS = 1e-05
HIGHEST = lax.Precision.HIGHEST
MESH = pl.DeviceIdType.MESH
F32 = jnp.float32
BF16 = jnp.bfloat16

NY, NZ, NX = 4, 8, 4
ROWS = 384
HALF = ROWS // 2
DB = 512
SUB = 128
CC = 1280
GC = 1024
G1, G2 = 512, 512
NH = 16
CHUNKS = 3

STREAMS = (
    ("c", 0, 0, 64, True),
    ("c", 1, 0, 64, False),
    ("g1", 0, 0, 64, True),
    ("g1", 1, 0, 64, True),
    ("g2", 0, 0, 64, True),
    ("g2", 1, 0, 64, False),
)
WIDTH = {"c": CC, "g1": G1, "g2": G2}
FIRST = {"c": GC, "g1": 0, "g2": G1}


def children(stream, dy, dz):
    along_z, flip = STREAMS[stream][4], stream in (2, 3)
    out = []
    if along_z:
        up, down = (3, 4) if flip else (4, 3)
        if dy == 0:
            if 0 <= dz < up:
                out.append((0, dz + 1, "z+"))
            if 0 <= -dz < down:
                out.append((0, dz - 1, "z-"))
            out.append((1, dz, "y"))
    else:
        if (dy, dz) == (0, 0):
            out.append((1, 0, "y"))
        up, down = (4, 3) if (dy == 0) != flip else (3, 4)
        if 0 <= dz < up:
            out.append((dy, dz + 1, "z+"))
        if 0 <= -dz < down:
            out.append((dy, dz - 1, "z-"))
    return out


STARTS = {20: (2, 3), 44: (4, 5)}


def plan():
    free = dict.fromkeys(("y", "z+", "z-", "x+", "x-"), 0.0)
    events, done, order, tick = [], {}, [], itertools.count()
    left = {"c": 30, "g1": 30, "g2": 30, "tok": 12}
    taken = {"ring": 0}
    rate = 45000.0

    def later(t, item):
        heapq.heappush(events, (t, next(tick), item))

    def send(t, link, size, item):
        free[link] = max(t, free[link]) + size / rate
        later(free[link] + 2.2, item)

    def ring(t, stream, dy, dz):
        kind, _, _, rows, _ = STREAMS[stream]
        for a, b, d in children(stream, dy, dz):
            send(t, d, rows * WIDTH[kind] * 2, ("ring", stream, a, b))

    piece = HALF * DB * 2
    for item, t in ((("tin", 0), 10.0), (("tin", 1), 12.0), (("own", 0), 1.5), (("fold", 1), 9.5)):
        later(t, item)
    fold_at = {"g1": 20.0, "g2": 21.0}

    tiles = (4, 0, 1, 2, 3)
    units = [(("norm", i), 0.65, [("tok",)] if i == 0 else [("norm", i - 1)]) for i in range(4)]
    units += [(("prefix",), 0.4, [("ex1",)]), (("back",), 0.4, [("ex2",)])]
    units += [(("ends",), 0.2, [("state", i) for i in range(4)])]
    units += [(("dt",), 1.2, [("c",), ("norm", 3)]), (("mats",), 5.2, [("dt",)])]
    units += [(("state", i), 0.7, [("conv", i), ("conv", 4), ("prep",)]) for i in range(4)]
    units += [(("conv", i), 0.5, [("halo", i), ("chan", i)]) for i in tiles]
    units += [(("chan", i), 0.1, [("ch", i)]) for i in tiles]
    units += [(("prep",), 0.8, [("raw",)])]
    units += [(("carry",), 1.4, [("ex3",)] + [("inner", q, j) for q in range(CHUNKS) for j in range(4)])]
    units += [(("gate", i), 0.35, [("carry",), ("g", i)]) for i in range(4)]
    units += [(("gmats", 0), 1.9, [("g1",), ("mats",)]), (("gmats", 1), 1.9, [("g2",), ("mats",)])]
    units += [(("inner", q, j), 0.45, [("state", i) for i in range(4)]) for q in range(CHUNKS) for j in range(4)]

    now = 0.0
    while events or units:
        ready = [e for e in events if e[0] <= now]
        if ready:
            e = min(ready)
            events.remove(e)
            item = e[2]
            if item[0] == "ring":
                order.append(item)
                stream = item[1]
                kind = STREAMS[stream][0]
                left[kind] -= 1
                if not left[kind]:
                    later(now + (1.5 if kind == "c" else 3.0), ("flag", (kind,)))
                ring(now, *item[1:])
                taken["ring"] += 1
                for late in STARTS.get(taken["ring"], ()):
                    order.append(("begin", late))
                    ring(max(now, fold_at[STREAMS[late][0]]), late, 0, 0)
            elif item[0] in ("own", "fold"):
                order.append(("begin", item[1]))
                ring(now, item[1], 0, 0)
            elif item[0] == "tin":
                order.append(item)
                k = item[1]
                for p in (0, 1):
                    send(now, "x+", piece, ("tr", -1, k, p))
                for p in (1, 0):
                    send(now, "x-", piece, ("tr", 1, k, p))
            elif item[0] == "tr":
                order.append(item)
                _, dx, k, p = item
                if dx < 0 and p == 0:
                    send(now, "x+", piece, ("ta", k, p))
                if dx > 0 and p == 1:
                    send(now, "x-", piece, ("ta", k, p))
                left["tok"] -= 1
            elif item[0] == "ta":
                order.append(item)
                left["tok"] -= 1
            elif item[0] == "flag":
                done[item[1]] = now
            if item[0] in ("tr", "ta") and not left["tok"]:
                done[("tok",)] = now
            now += 0.05
            continue
        todo = [u for u in units if all(n in done for n in u[2])]
        if todo:
            unit = todo[0]
            units.remove(unit)
            name = unit[0]
            order.append(name)
            now += unit[1]
            done[name] = now
            if name[0] == "mats":
                for i, tile in enumerate(tiles):
                    later(now + max(i - 1, 0), ("flag", ("ch", tile)))
                    later(now + max(i - 1, 0) + 1.0, ("flag", ("halo", tile)))
            if name[0] == "dt":
                later(now + 2.5, ("flag", ("raw",)))
            if name[0] == "gmats":
                for i in (0, 1):
                    later(now + 4.5, ("flag", ("g", 2 * name[1] + i)))
            if name[0] in ("state", "back"):
                size = 74000 if name[0] == "state" else 295000
                for link in ("z+", "z-"):
                    free[link] = max(now, free[link]) + size / rate
                if name[0] == "back":
                    later(max(free["z+"], free["z-"]) + 3.0, ("flag", ("ex3",)))
            if name[0] == "ends":
                later(max(free["z+"], free["z-"], now) + 3.0, ("flag", ("ex1",)))
            if name[0] == "prefix":
                later(now + 4.0, ("flag", ("ex2",)))
            continue
        if not events:
            raise ValueError("stuck")
        now = min(events)[0]
    return order


PLAN = plan()


def number(dy, dz):
    return dy * NZ + dz % NZ


def softplus(v):
    return jnp.maximum(v, 0.0) + jnp.log1p(jnp.exp(-jnp.abs(v)))


def silu(v):
    return v / (1.0 + jnp.exp(-v))


def dot_nt(a, b):
    return lax.dot_general(a, b, (((1,), (1,)), ((), ())), preferred_element_type=F32)


def dot_tn(a, b):
    return lax.dot_general(a, b, (((0,), (0,)), ((), ())), preferred_element_type=F32)


def kernel(
    tok_in, w_in, w_dt, w_out, norm_gain, dt_bias, a_log, d_skip, conv_w, conv_b, gate_gain,
    out_ref,
    tok, xn, wc, wg1, wg2, wd, wo, ch, gs, raw,
    chf, halo_out, halo_in, cv, ybuf, tt, ct, fs, scores,
    e_out, d_out, e_in, d_in, pre, row_out, rowd_out, row_in, rowd_in, back_out, sin,
    no, sib_out, sib_in, part, far_out, far_in, near_out, near_in,
    load_sem, w_send, w_recv, f_send, f_recv, d_send, d_recv, t_send, t_recv, c_send, c_recv, h_send, h_recv,
    s_send, s_recv, r_send, r_recv, b_send, b_recv, o_send, o_recv, x_send, x_recv,
):
    s = lax.axis_index("seq")
    hd = lax.axis_index("head")
    y, z = lax.div(s, NZ), lax.rem(s, NZ)
    x, c = lax.div(hd, 2), lax.rem(hd, 2)
    kind_of_row = lax.div(y, 2)
    home = c == kind_of_row
    away = c != kind_of_row

    def at_yz(dy, dz):
        return lax.rem(y + dy + 2 * NY, NY) * NZ + lax.rem(z + dz + 2 * NZ, NZ)

    def head_of(dx, core):
        return lax.rem(x + dx + NX, NX) * 2 + core

    other = (NY - 1 - y) * NZ + z
    mate = (y + 1 - 2 * lax.rem(y, 2)) * NZ + z
    sibling = (s, x * 2 + (1 - c))
    plus, minus = (s, head_of(1, c)), (s, head_of(-1, c))
    lent = lax.select(home, 0, 1)
    halo_to = (lax.rem(lax.select(home, s, other) + 1, NY * NZ), x * 2 + lax.select(home, c, 1 - c))
    earlier = lax.rem(s + NY * NZ - 1, NY * NZ)
    earlier_row = lax.div(earlier, NZ)
    earlier_home = lax.div(earlier_row, 2) == c
    halo_from = (
        lax.select(earlier_home, earlier, (NY - 1 - earlier_row) * NZ + lax.rem(earlier, NZ)),
        x * 2 + lax.select(earlier_home, c, 1 - c),
    )
    target = {"y": (mate, hd), "z+": (at_yz(0, 1), hd), "z-": (at_yz(0, -1), hd)}
    z_peers = [(at_yz(0, k), hd) for k in range(1, NZ)]
    y_peers = [(at_yz(k, 0), hd) for k in range(1, NY)]
    swap = (other, x * 2 + (1 - c))
    sent, sent_if = [], []

    def remote(src, dst, send, recv, where):
        return pltpu.make_async_remote_copy(
            src_ref=src, dst_ref=dst, send_sem=send, recv_sem=recv, device_id=where, device_id_type=MESH
        )

    def push(src, dst, send, recv, where):
        copy = remote(src, dst, send, recv, where)
        copy.start()
        sent.append(copy)

    def push_if(condition, src, dst, send, recv, where):
        copy = remote(src, dst, send, recv, where)
        pl.when(condition)(copy.start)
        sent_if.append((condition, copy))

    def arrived(ref, recv):
        remote(ref, ref, recv, recv, sibling).wait_recv()

    def arrived_if(condition, ref, recv):
        pl.when(condition)(remote(ref, ref, recv, recv, sibling).wait_recv)

    held = {"c": wc, "g1": wg1, "g2": wg2}

    def cols_in(kind):
        return pl.ds(FIRST[kind], WIDTH[kind])

    def row_of(dy, dz, partner):
        row = y + dy * (1 - 2 * lax.rem(y, 2))
        row = NY - 1 - row if partner else row
        return (row * NZ + lax.rem(z - dz + NZ, NZ)) * SUB

    def block(stream, dy, dz, core):
        kind, partner, first, rows, _ = STREAMS[stream]
        base = row_of(dy, dz, partner) + 64 * core + first
        return held[kind].at[pl.ds(pl.multiple_of(base, 16), rows), :]

    def dt_block(dy, dz, partner):
        return wd.at[:, pl.ds(pl.multiple_of(row_of(dy, dz, partner), SUB), SUB)]

    own_rows = pl.ds(pl.multiple_of(row_of(0, 0, 0), SUB), SUB)
    kinds = ("c", "g1", "g2")
    loads = {k: pltpu.make_async_copy(w_in.at[:, cols_in(k)], held[k].at[own_rows, :], load_sem.at[i]) for i, k in enumerate(kinds)}
    loads["dt"] = pltpu.make_async_copy(w_dt, wd.at[:, own_rows], load_sem.at[3])
    own_cols = pl.ds(pl.multiple_of(c * DB, DB), DB)
    sib_cols = pl.ds(pl.multiple_of((1 - c) * DB, DB), DB)
    loads["tok"] = pltpu.make_async_copy(tok_in, tok.at[x, :, own_cols], load_sem.at[4])
    wo_load = pltpu.make_async_copy(w_out, wo, load_sem.at[5])

    @pl.when(home)
    def _():
        for key in ("c", "dt", "tok", "g1", "g2"):
            loads[key].start()

    wo_load.start()

    barrier = pltpu.get_barrier_semaphore()
    peers = z_peers + y_peers + [plus, minus, sibling, halo_to, halo_from, swap]
    for peer in peers:
        pl.semaphore_signal(barrier, inc=1, device_id=peer, device_id_type=MESH)
    pl.semaphore_wait(barrier, len(peers))

    half = [pl.ds(0, HALF), pl.ds(HALF, HALF)]
    here = [(other, x * 2), (other, x * 2 + 1)]

    def fold(kind, index):
        push_if(home, w_in.at[:, cols_in(kind)], held[kind].at[own_rows, :], f_send.at[0, index], f_recv.at[0, index], sibling)
        for core in (0, 1):
            rows = pl.ds(64 * core, 64)
            there = pl.ds(pl.multiple_of(row_of(0, 0, 0) + 64 * core, 16), 64)
            push_if(
                away, w_in.at[rows, cols_in(kind)], held[kind].at[there, :],
                f_send.at[1 + core, index], f_recv.at[1, index], here[core],
            )

    def fold_dt():
        push_if(home, w_dt, wd.at[:, own_rows], f_send.at[0, 3], f_recv.at[0, 3], sibling)
        for core in (0, 1):
            push_if(away, w_dt, wd.at[:, own_rows], f_send.at[1 + core, 3], f_recv.at[1, 3], here[core])

    fold("c", 0)
    fold_dt()
    for k in (0, 1):
        rows = half[k]
        into = tok.at[x, rows, own_cols]
        push_if(away, tok_in.at[rows, :], into, t_send.at[14 + k], t_recv.at[14 + k], sibling)
        push_if(home, tok_in.at[rows, :], into, t_send.at[12 + k], t_recv.at[12 + k], (other, hd))
        push_if(away, tok_in.at[rows, :], into, t_send.at[12 + k], t_recv.at[14 + k], swap)
    fold("g1", 1)
    fold("g2", 2)

    def own_ready(kind, index):
        @pl.when(home)
        def _():
            loads[kind].wait()

        ref = wd.at[:, own_rows] if kind == "dt" else held[kind].at[own_rows, :]
        arrived_if(away, ref, f_recv.at[0, index])

    def partner_ready(kind, index):
        base = row_of(0, 0, 1)
        if kind == "dt":
            arrived(dt_block(0, 0, 1), f_recv.at[1, index])
        else:
            arrived(held[kind].at[pl.ds(pl.multiple_of(base + 64 * c, 16), 64), :], f_recv.at[1, index])

    def spread(stream, dy, dz):
        piece = block(stream, dy, dz, c)
        for a, b, d in children(stream, dy, dz):
            k = number(a, b)
            push(piece, piece, w_send.at[stream, k], w_recv.at[stream, k], target[d])
            if stream < 2:
                small = dt_block(dy, dz, stream)
                push(small, small, w_send.at[6 + stream, k], w_recv.at[6 + stream, k], target[d])
        if (dy, dz) != (0, 0) or STREAMS[stream][1]:
            k = number(dy, dz)
            push(piece, piece, d_send.at[stream, k], d_recv.at[stream, k], sibling)

    def all_here(streams):
        for stream in streams:
            for dy in (0, 1):
                for dz in range(NZ):
                    if (dy, dz) != (0, 0) or STREAMS[stream][1]:
                        arrived(block(stream, dy, dz, 1 - c), d_recv.at[stream, number(dy, dz)])

    def begin(stream):
        kind, partner = STREAMS[stream][:2]
        index = kinds.index(kind)
        if partner:
            partner_ready(kind, index)
            if stream == 1:
                partner_ready("dt", 3)
        else:
            own_ready(kind, index)
            if stream == 0:
                own_ready("dt", 3)
        spread(stream, 0, 0)

    def ring(stream, dy, dz):
        k = number(dy, dz)
        arrived(block(stream, dy, dz, c), w_recv.at[stream, k])
        if stream < 2:
            arrived(dt_block(dy, dz, stream), w_recv.at[6 + stream, k])
        spread(stream, dy, dz)

    def tok_piece(dx, k, p):
        return tok.at[lax.rem(x + dx + NX, NX), half[k], own_cols if p == 0 else sib_cols]

    def tok_in_here(k):
        if k == 0:

            @pl.when(home)
            def _():
                loads["tok"].wait()

        arrived_if(away, tok_piece(0, k, 0), t_recv.at[12 + k])
        arrived(tok_piece(0, k, 1), t_recv.at[14 + k])
        for p in (0, 1):
            piece = tok_piece(0, k, p)
            push(piece, piece, t_send.at[k * 2 + p], t_recv.at[k * 2 + p], plus)
        for p in (1, 0):
            piece = tok_piece(0, k, p)
            push(piece, piece, t_send.at[4 + k * 2 + p], t_recv.at[4 + k * 2 + p], minus)

    def tok_relay(dx, k, p):
        piece = tok_piece(dx, k, p)
        index = (0 if dx < 0 else 4) + k * 2 + p
        arrived(piece, t_recv.at[index])
        if dx < 0 and p == 0:
            push(piece, piece, t_send.at[8 + k], t_recv.at[8 + k], plus)
        if dx > 0 and p == 1:
            push(piece, piece, t_send.at[10 + k], t_recv.at[10 + k], minus)

    def tok_far(k, p):
        arrived(tok_piece(2, k, p), t_recv.at[(8 if p == 0 else 10) + k])

    def norm_rows(i, carry):
        rows = pl.ds(pl.multiple_of(i * 32, 32), 32)
        total = jnp.zeros((32, 1), F32)
        for h in range(8):
            v = tok[h // 2, rows, (h % 2) * DB : (h % 2 + 1) * DB].astype(F32)
            total = total + jnp.sum(v * v, axis=1, keepdims=True)
        scale = lax.rsqrt(total / (8 * DB) + EPS)
        for h in range(8):
            cols = slice((h % 2) * DB, (h % 2 + 1) * DB)
            v = tok[h // 2, rows, cols].astype(F32)
            xn[rows, h * DB : (h + 1) * DB] = (v * scale * norm_gain[:, h * DB : (h + 1) * DB]).astype(BF16)
        return carry

    def norm(i):
        lax.fori_loop(i * 3, i * 3 + 3, norm_rows, 0)

    def project(weights, first, width):
        cols = pl.ds(first, width)
        return jnp.dot(xn[...], weights[:, cols], preferred_element_type=F32).astype(BF16)

    def ship(buffer, tile, index):
        push_if(away, buffer.at[1, tile], buffer.at[0, tile], c_send.at[index], c_recv.at[index], swap)

    pending = []

    def channel_copies(tile):
        return (
            remote(halo_out.at[tile], halo_in.at[tile], h_send.at[tile], h_recv.at[tile], halo_to),
            remote(ch.at[1, tile], ch.at[0, tile], c_send.at[tile], c_recv.at[tile], swap),
        )

    def send_channels(tile):
        halo, rest = channel_copies(tile)
        halo.start()
        pl.when(away)(rest.start)

    def mats():
        all_here((0, 1))

        def one(i, carry):
            tile = lax.rem(i + 4, 5)

            @pl.when(i > 0)
            def _():
                send_channels(lax.rem(i + 3, 5))

            value = project(wc, pl.multiple_of(tile * 256, 256), 256)
            ch[lent, tile] = value
            halo_out[tile] = value[ROWS - 16 :, :]
            return carry

        lax.fori_loop(0, 5, one, 0)
        for tile in range(5):
            halo, rest = channel_copies(tile)
            sent.append(halo)
            sent_if.append((away, rest))
        pending.append(lambda: send_channels(3))

    def dt():
        raw[lent, 0] = dot_nt(wd[...], xn[...])
        pending.append(lambda: ship(raw, 0, 5))

    def gate_copy(tile):
        return remote(gs.at[1, tile], gs.at[0, tile], c_send.at[6 + tile], c_recv.at[6 + tile], swap)

    def gmats(second):
        all_here((4, 5) if second else (2, 3))
        base = 2 * second
        value = project(wg2 if second else wg1, 0, 512)
        for tile in (0, 1):
            gs[lent, base + tile] = value[:, tile * 256 : (tile + 1) * 256]
            sent_if.append((away, gate_copy(base + tile)))

        @pl.when(away)
        def _():
            gate_copy(base).start()
            gate_copy(base + 1).start()

    def chan(tile):
        arrived_if(away, ch.at[0, tile], c_recv.at[tile])
        chf[8:, tile * 256 : (tile + 1) * 256] = ch[0, tile].astype(F32)

    def column_of(ref):
        wide = jnp.concatenate([ref[...], jnp.zeros((1, 128 - NH), F32)], axis=1)
        return jnp.transpose(jnp.broadcast_to(wide, (128, 128)))[:NH, :1]

    row_id = lax.broadcasted_iota(jnp.int32, (128, 128), 0)
    lane_id = lax.broadcasted_iota(jnp.int32, (128, 128), 1)
    first_half = lane_id < 64
    upper_rows = row_id < 64

    def prep():
        arrived_if(away, raw.at[0, 0], c_recv.at[5])
        step = softplus(raw[0, 0] + column_of(dt_bias))
        decay = -jnp.exp(column_of(a_log)) * step
        upper = jnp.where(row_id <= lane_id, 1.0, 0.0).astype(F32)
        for q in range(CHUNKS):
            span = slice(q * 128, (q + 1) * 128)
            cum = jnp.dot(decay[:, span], upper, precision=HIGHEST, preferred_element_type=F32)
            to_end = jnp.exp(cum[:, 127:128] - cum) * step[:, span]
            ct[q] = cum
            stacked = jnp.concatenate(
                [cum, to_end, step[:, span], jnp.exp(cum), jnp.zeros((64, 128), F32)], axis=0
            )
            tt[q] = jnp.transpose(stacked)
        d_out[...] = jnp.broadcast_to(tt[0, 127:128, :] + tt[1, 127:128, :] + tt[2, 127:128, :], (8, 128))
        d_in[z] = d_out[...]

    def conv(tile):
        arrived(halo_in.at[tile], h_recv.at[tile])
        wide = slice(tile * 256, (tile + 1) * 256)
        chf[:8, wide] = jnp.where(s > 0, halo_in[tile, 8:16, :].astype(F32), 0.0)
        for cols in (slice(tile * 256, tile * 256 + 128), slice(tile * 256 + 128, tile * 256 + 256)):
            for q in range(CHUNKS):
                total = conv_b[:, cols] + jnp.zeros((128, 128), F32)
                for k in range(4):
                    total = total + conv_w[k, :, cols] * chf[q * 128 + 5 + k : q * 128 + 133 + k, cols]
                cv[q * 128 : (q + 1) * 128, cols] = silu(total).astype(BF16)

    def pair_cols(table, base, j):
        return jnp.where(
            first_half, table[:, base + 2 * j : base + 2 * j + 1], table[:, base + 2 * j + 1 : base + 2 * j + 2]
        )

    def pair_rows(row, j):
        return jnp.where(upper_rows, jnp.exp(row[:, 2 * j : 2 * j + 1]), jnp.exp(row[:, 2 * j + 1 : 2 * j + 2]))

    def end_states(tile):
        for j in (2 * tile, 2 * tile + 1):
            cols = slice(j * 128, (j + 1) * 128)
            for q in range(CHUNKS):
                span = slice(q * 128, (q + 1) * 128)
                weighted = (cv[span, cols].astype(F32) * pair_cols(tt[q], 16, j)).astype(BF16)
                fs[q, cols, :] = dot_tn(weighted, cv[span, 1024:1152])
            total = fs[1, cols, :] + pair_rows(tt[1, 127:128, :], j) * fs[0, cols, :]
            e_out[j] = (fs[2, cols, :] + pair_rows(tt[2, 127:128, :], j) * total).astype(BF16)

        def go():
            for j in (2 * tile, 2 * tile + 1):
                peer = (y * NZ + j, hd)
                push_if(z != j, e_out.at[j], e_in.at[z], s_send.at[0, j], s_recv.at[0, z], peer)
                push_if(z != j, d_out, d_in.at[z], s_send.at[1, j], s_recv.at[1, z], peer)

        pending.append(go)

    def inner(q, part_of):
        span = slice(q * 128, (q + 1) * 128)
        if part_of == 0:
            scores[...] = jnp.where(row_id >= lane_id, dot_nt(cv[span, 1152:1280], cv[span, 1024:1152]), 0.0)
        table = tt[q]
        for j in (2 * part_of, 2 * part_of + 1):
            cols = slice(j * 128, (j + 1) * 128)
            v = cv[span, cols].astype(F32)
            stepped = v * pair_cols(table, 32, j)
            values = jnp.concatenate(
                [jnp.where(first_half, stepped, 0.0), jnp.where(first_half, 0.0, stepped)], axis=0
            ).astype(BF16)
            weights = []
            for h in (2 * j, 2 * j + 1):
                gap = jnp.minimum(table[:, h : h + 1] - ct[q, h : h + 1, :], 0.0)
                weights.append((scores[...] * jnp.exp(gap)).astype(BF16))
            within = jnp.dot(jnp.concatenate(weights, axis=1), values, preferred_element_type=F32)
            skip = jnp.where(first_half[:1], d_skip[:, 2 * j : 2 * j + 1], d_skip[:, 2 * j + 1 : 2 * j + 2])
            ybuf[span, cols] = within + skip * v

    def ends():
        e_in[z] = e_out[z]

    lane_row = lax.broadcasted_iota(jnp.int32, (1, 128), 1)

    def pick(row, lane):
        return jnp.sum(jnp.where(lane_row == lane, row, 0.0), axis=1, keepdims=True)

    def factor(pair):
        return jnp.where(upper_rows[:, :1], jnp.exp(pair[0]), jnp.exp(pair[1]))

    before = []

    def prefix():
        for k in range(1, NZ):
            source = lax.rem(z + NZ - k, NZ)
            arrived(e_in.at[source], s_recv.at[0, source])
            arrived(d_in.at[source], s_recv.at[1, source])
        running = jnp.zeros((128, 128), F32)
        gone = (jnp.zeros((1, 1), F32), jnp.zeros((1, 1), F32))
        for k in range(NZ):
            pre[k] = running
            before.append(gone)
            row = d_in[k, :1, :]
            pair = (pick(row, 2 * z), pick(row, 2 * z + 1))
            running = factor(pair) * running + e_in[k].astype(F32)
            gone = (gone[0] + pair[0], gone[1] + pair[1])
        row_out[...] = running.astype(BF16)
        rowd_out[...] = jnp.broadcast_to(jnp.where(lane_row == 0, gone[0], gone[1]), (8, 128))
        row_in[y] = running.astype(BF16)
        rowd_in[y] = jnp.broadcast_to(jnp.where(lane_row == 0, gone[0], gone[1]), (8, 128))

        def go():
            for k in range(1, NY):
                push(row_out, row_in.at[y], r_send.at[0, k], r_recv.at[0, k], y_peers[k - 1])
                push(rowd_out, rowd_in.at[y], r_send.at[1, k], r_recv.at[1, k], y_peers[k - 1])

        pending.append(go)

    def back():
        for k in range(1, NY):
            source = lax.rem(y + NY - k, NY)
            arrived(row_in.at[source], r_recv.at[0, k])
            arrived(rowd_in.at[source], r_recv.at[1, k])
        entering = jnp.zeros((128, 128), F32)
        for k in range(NY):
            row = rowd_in[k, :1, :]
            moved = factor((row[:, 0:1], row[:, 1:2])) * entering + row_in[k].astype(F32)
            entering = jnp.where(k < y, moved, entering)
        for k in range(NZ):
            back_out[k] = (factor(before[k]) * entering + pre[k]).astype(BF16)
        sin[z] = back_out[z]

        def go():
            for k in range(1, NZ):
                peer = lax.rem(z + k, NZ)
                push(back_out.at[peer], sin.at[z], b_send.at[k], b_recv.at[k], z_peers[k - 1])

        pending.append(go)

    def carry():
        for k in range(1, NZ):
            arrived(sin.at[lax.rem(z + NZ - k, NZ)], b_recv.at[k])
        for j in range(8):
            cols = slice(j * 128, (j + 1) * 128)
            entering = sin[j].astype(F32)
            for q in range(CHUNKS):
                span = slice(q * 128, (q + 1) * 128)
                across = dot_nt(cv[span, 1152:1280], entering.astype(BF16))
                ybuf[span, cols] += pair_cols(tt[q], 48, j) * across
                if q < CHUNKS - 1:
                    entering = pair_rows(tt[q, 127:128, :], j) * entering + fs[q, cols, :]

    squares = [jnp.zeros((ROWS, 1), F32)]

    def gate(tile):
        cols = slice(tile * 256, (tile + 1) * 256)
        arrived_if(away, gs.at[0, tile], c_recv.at[6 + tile])
        gated = ybuf[:, cols] * silu(gs[0, tile].astype(F32))
        ybuf[:, cols] = gated
        squares[0] = squares[0] + jnp.sum(gated * gated, axis=1, keepdims=True)

    steps = {
        "begin": begin, "ring": ring, "tin": tok_in_here, "tr": tok_relay, "ta": tok_far, "norm": norm, "mats": mats,
        "dt": dt, "gmats": gmats, "chan": chan, "prep": prep, "conv": conv, "state": end_states, "inner": inner,
        "ends": ends, "prefix": prefix, "back": back, "carry": carry, "gate": gate,
    }
    for step in PLAN:
        later, pending[:] = list(pending), []
        for go in later:
            go()
        steps[step[0]](*step[1:])
    for go in pending:
        go()
    scale = lax.rsqrt(squares[0] / GC + EPS)

    def norm_tile(i, carry):
        cols = pl.ds(pl.multiple_of(i * 128, 128), 128)
        no[:, cols] = (ybuf[:, cols] * scale * gate_gain[:, cols]).astype(BF16)
        return carry

    lax.fori_loop(0, 8, norm_tile, 0)
    wo_load.wait()

    def term(dx, core, into):
        cols = pl.ds(pl.multiple_of(head_of(dx, core) * DB, DB), DB)
        into[...] = jnp.dot(no[...], wo[:, cols], preferred_element_type=F32).astype(into.dtype)

    top, low = half

    def to_sibling(r):
        term(r, 1 - c, sib_out.at[r])

    def keep(r):
        term(r, c, part.at[r])

    def send_sibling(r):
        push(sib_out.at[r], sib_in.at[r], o_send.at[r], o_recv.at[r], sibling)

    def chip_sum(r, rows):
        return part[r, rows, :] + sib_in[r, rows, :].astype(F32)

    to_sibling(2)
    keep(2)
    send_sibling(2)
    to_sibling(1)
    to_sibling(3)
    send_sibling(1)
    keep(1)
    send_sibling(3)
    arrived(sib_in.at[2], o_recv.at[2])
    far_out[...] = chip_sum(2, slice(None)).astype(BF16)
    keep(3)
    push(far_out.at[top, :], far_in.at[0], x_send.at[0], x_recv.at[0], plus)
    push(far_out.at[low, :], far_in.at[1], x_send.at[1], x_recv.at[1], minus)
    arrived(sib_in.at[1], o_recv.at[1])
    near_out[0, low, :] = chip_sum(1, low).astype(BF16)
    arrived(sib_in.at[3], o_recv.at[3])
    near_out[1, top, :] = chip_sum(3, top).astype(BF16)
    push(near_out.at[0, low, :], near_in.at[0, low, :], x_send.at[2], x_recv.at[2], plus)
    to_sibling(0)
    push(near_out.at[1, top, :], near_in.at[1, top, :], x_send.at[3], x_recv.at[3], minus)
    keep(0)
    send_sibling(0)
    arrived(far_in.at[0], x_recv.at[0])
    near_out[0, top, :] = (chip_sum(1, top) + far_in[0].astype(F32)).astype(BF16)
    push(near_out.at[0, top, :], near_in.at[0, top, :], x_send.at[4], x_recv.at[4], plus)
    arrived(far_in.at[1], x_recv.at[1])
    near_out[1, low, :] = (chip_sum(3, low) + far_in[1].astype(F32)).astype(BF16)
    push(near_out.at[1, low, :], near_in.at[1, low, :], x_send.at[5], x_recv.at[5], minus)
    arrived(sib_in.at[0], o_recv.at[0])
    part[0] = chip_sum(0, slice(None))
    arrived(near_in.at[0, low, :], x_recv.at[2])
    arrived(near_in.at[1, top, :], x_recv.at[3])
    arrived(near_in.at[0, top, :], x_recv.at[4])
    arrived(near_in.at[1, low, :], x_recv.at[5])
    out_ref[...] = (part[0] + near_in[0].astype(F32) + near_in[1].astype(F32)).astype(BF16)
    for copy in sent:
        copy.wait_send()
    for condition, copy in sent_if:
        pl.when(condition)(copy.wait_send)


def body(tokens, norm_gain, w_in, w_dt, dt_bias, a_log, d_skip, conv_w, conv_b, gate_gain, w_out):
    any_space = pl.BlockSpec(memory_space=pl.ANY)
    vmem = pl.BlockSpec(memory_space=pltpu.VMEM)
    dma = pltpu.SemaphoreType.DMA

    def buf(*shape, dtype=BF16):
        return pltpu.VMEM(shape, dtype)

    scratch = [
        buf(NX, ROWS, 2 * DB), buf(ROWS, 4096), buf(4096, CC), buf(4096, G1), buf(4096, G2),
        buf(NH, 4096), buf(GC, 4096), buf(2, 5, ROWS, 256), buf(2, 4, ROWS, 256),
        buf(2, 1, NH, ROWS, dtype=F32),
        buf(ROWS + 8, CC, dtype=F32), buf(5, 16, 256), buf(5, 16, 256), buf(ROWS, CC), buf(ROWS, GC, dtype=F32),
        buf(CHUNKS, 128, 128, dtype=F32), buf(CHUNKS, NH, 128, dtype=F32), buf(CHUNKS, GC, 128, dtype=F32), buf(128, 128, dtype=F32),
        buf(8, 128, 128), buf(8, 128, dtype=F32), buf(8, 128, 128), buf(8, 8, 128, dtype=F32),
        buf(8, 128, 128, dtype=F32),
        buf(128, 128), buf(8, 128, dtype=F32), buf(NY, 128, 128), buf(NY, 8, 128, dtype=F32),
        buf(8, 128, 128), buf(8, 128, 128),
        buf(ROWS, GC), buf(4, ROWS, DB), buf(4, ROWS, DB), buf(4, ROWS, DB, dtype=F32),
        buf(ROWS, DB), buf(2, ROWS // 2, DB), buf(2, ROWS, DB), buf(2, ROWS, DB),
        dma((6,)), dma((8, 16)), dma((8, 16)), dma((3, 4)), dma((2, 4)), dma((6, 16)), dma((6, 16)),
        dma((16,)), dma((16,)), dma((10,)), dma((10,)), dma((5,)), dma((5,)),
        dma((2, NZ)), dma((2, NZ)), dma((2, NY)), dma((2, NY)), dma((NZ,)), dma((NZ,)),
        dma((4,)), dma((4,)), dma((6,)), dma((6,)),
    ]
    return pl.pallas_call(
        kernel,
        out_shape=jax.ShapeDtypeStruct((ROWS, DB), BF16),
        in_specs=[any_space] * 4 + [vmem] * 7,
        out_specs=vmem,
        scratch_shapes=scratch,
        compiler_params=pltpu.CompilerParams(
            collective_id=0, has_side_effects=True, vmem_limit_bytes=64 * 1024 * 1024 - 65536
        ),
    )(
        tokens, w_in.reshape(SUB, GC + CC), w_dt.T, w_out.reshape(GC, 4096),
        norm_gain.reshape(1, 4096), dt_bias.reshape(1, NH), a_log.reshape(1, NH), d_skip.reshape(1, NH),
        conv_w, conv_b, gate_gain,
    )


def solution(mesh):
    in_specs = (
        P("seq", "head"), P(), P("seq", "head", None), P("seq", "head"), P("head"), P("head"), P("head"),
        P(None, "head", None), P("head", None), P("head", None), P("head", None, None),
    )
    return jax.shard_map(body, mesh=mesh, in_specs=in_specs, out_specs=P("seq", "head"), check_vma=False)
```

time: 162 us -> 129 us (0.80)
  Pallas kernels: 158 us -> 128 us
    pallas_call x1, Pallas kernels: 158 us -> 128 us  [body(): pl.pallas_call(kernel, out_shape=jax.ShapeDtypeStruct((ROWS, DB), BF16),...]
where the time goes in v2:
time: 129 us
  Pallas kernels  128 us (99%)
  local copies, waits for them, and re-layouts  1.77 us (1%)
    pallas_call x1, Pallas kernels, body(): pl.pallas_call(kernel, out_shape=jax.ShapeDtypeStruct((ROWS, DB), BF16),...  128 us

profile of v2, /device:TPU:24, one launch (start us, length us, event | category | flops | bytes accessed | tf_op | source)
XLA Modules:
  0.0 129.3 jit_solution(7450241955568729105)
XLA Ops:
  0.0 127.5 %shard_map.109 = bf16[384,512]{1,0:T(8,128)(2,1)} custom-call(bf16[384,512]{1,0:T(8,128)(2,1)} %tok_in.1, bf16[128,2304]{1,0:T(8,128)(2,1)} %bitcast.8, bf16[16,128]{1,0:T(8,128)(2,1)} %bitcast.10, bf16[1024,4096]{1,0:T(8,128)(2,1)} %bitcast.7, f32[1,4096]{1,0:T(1,128)} %bitcast.9, f32[1,16]{1,0:T(1,128)} %bitcast.11, f32[1,16]{1,0:T(1,128)} %bitcast.12, ...), custom_call_target="tpu_custom_call" | custom-call | tf_op jit(solution)/shard_map/pallas_call | solution.py:777
  127.5 1.8 %copy.13 = bf16[384,512]{1,0:T(8,128)(2,1)} copy(bf16[384,512]{1,0:T(8,128)(2,1)} %shard_map.109) | data formatting | bytes 786432

commit v3 on v2

--- a/solution.py
+++ b/solution.py
@@ -59,7 +59,9 @@
     return out
 
 
-STARTS = {20: (2, 3), 44: (4, 5)}
+STARTS = {26: (2, 3), 32: (4, 5)}
+EX, HAND = (1.0, 3.5, 1.0), {"c": 1.5, "g1": 3.0, "g2": 3.0}
+TIN, FOLD, XRATE = (12.0, 14.0), 10.0, (80000.0, 45000.0)
 
 
 def plan():
@@ -72,8 +74,8 @@
     def later(t, item):
         heapq.heappush(events, (t, next(tick), item))
 
-    def send(t, link, size, item):
-        free[link] = max(t, free[link]) + size / rate
+    def send(t, link, size, item, speed=45000.0):
+        free[link] = max(t, free[link]) + size / speed
         later(free[link] + 2.2, item)
 
     def ring(t, stream, dy, dz):
@@ -82,7 +84,7 @@
             send(t, d, rows * WIDTH[kind] * 2, ("ring", stream, a, b))
 
     piece = HALF * DB * 2
-    for item, t in ((("tin", 0), 10.0), (("tin", 1), 12.0), (("own", 0), 1.5), (("fold", 1), 9.5)):
+    for item, t in ((("tinh", 0), 3.0), (("tinh", 1), 3.5), (("tin", 0), TIN[0]), (("tin", 1), TIN[1]), (("own", 0), 1.5), (("fold", 1), FOLD)):
         later(t, item)
     fold_at = {"g1": 20.0, "g2": 21.0}
 
@@ -90,14 +92,14 @@
     units = [(("norm", i), 0.65, [("tok",)] if i == 0 else [("norm", i - 1)]) for i in range(4)]
     units += [(("prefix",), 0.4, [("ex1",)]), (("back",), 0.4, [("ex2",)])]
     units += [(("ends",), 0.2, [("state", i) for i in range(4)])]
-    units += [(("dt",), 1.2, [("c",), ("norm", 3)]), (("mats",), 5.2, [("dt",)])]
+    units += [(("dt",), 1.2, [("c",), ("norm", 3)]), (("mats", 0), 3.6, [("dt",)]), (("mats", 1), 1.9, [("mats", 0)])]
     units += [(("state", i), 0.7, [("conv", i), ("conv", 4), ("prep",)]) for i in range(4)]
     units += [(("conv", i), 0.5, [("halo", i), ("chan", i)]) for i in tiles]
     units += [(("chan", i), 0.1, [("ch", i)]) for i in tiles]
     units += [(("prep",), 0.8, [("raw",)])]
     units += [(("carry",), 1.4, [("ex3",)] + [("inner", q, j) for q in range(CHUNKS) for j in range(4)])]
     units += [(("gate", i), 0.35, [("carry",), ("g", i)]) for i in range(4)]
-    units += [(("gmats", 0), 1.9, [("g1",), ("mats",)]), (("gmats", 1), 1.9, [("g2",), ("mats",)])]
+    units += [(("gmats", 0), 1.9, [("g1",), ("mats", 1)]), (("gmats", 1), 1.9, [("g2",), ("mats", 1)])]
     units += [(("inner", q, j), 0.45, [("state", i) for i in range(4)]) for q in range(CHUNKS) for j in range(4)]
 
     now = 0.0
@@ -113,7 +115,7 @@
                 kind = STREAMS[stream][0]
                 left[kind] -= 1
                 if not left[kind]:
-                    later(now + (1.5 if kind == "c" else 3.0), ("flag", (kind,)))
+                    later(now + HAND[kind], ("flag", (kind,)))
                 ring(now, *item[1:])
                 taken["ring"] += 1
                 for late in STARTS.get(taken["ring"], ()):
@@ -122,20 +124,22 @@
             elif item[0] in ("own", "fold"):
                 order.append(("begin", item[1]))
                 ring(now, item[1], 0, 0)
+            elif item[0] == "tinh":
+                order.append(item)
             elif item[0] == "tin":
                 order.append(item)
                 k = item[1]
                 for p in (0, 1):
-                    send(now, "x+", piece, ("tr", -1, k, p))
+                    send(now, "x+", piece, ("tr", -1, k, p), XRATE[0])
                 for p in (1, 0):
-                    send(now, "x-", piece, ("tr", 1, k, p))
+                    send(now, "x-", piece, ("tr", 1, k, p), XRATE[0])
             elif item[0] == "tr":
                 order.append(item)
                 _, dx, k, p = item
                 if dx < 0 and p == 0:
-                    send(now, "x+", piece, ("ta", k, p))
+                    send(now, "x+", piece, ("ta", k, p), XRATE[1])
                 if dx > 0 and p == 1:
-                    send(now, "x-", piece, ("ta", k, p))
+                    send(now, "x-", piece, ("ta", k, p), XRATE[1])
                 left["tok"] -= 1
             elif item[0] == "ta":
                 order.append(item)
@@ -155,9 +159,10 @@
             now += unit[1]
             done[name] = now
             if name[0] == "mats":
-                for i, tile in enumerate(tiles):
-                    later(now + max(i - 1, 0), ("flag", ("ch", tile)))
-                    later(now + max(i - 1, 0) + 1.0, ("flag", ("halo", tile)))
+                for i, tile in enumerate((2, 3) if name[1] else (4, 0, 1)):
+                    wait = 3.0 + 1.8 * i if name[1] else 2.0 + i
+                    later(now + wait, ("flag", ("ch", tile)))
+                    later(now + wait + 0.5, ("flag", ("halo", tile)))
             if name[0] == "dt":
                 later(now + 2.5, ("flag", ("raw",)))
             if name[0] == "gmats":
@@ -168,11 +173,11 @@
                 for link in ("z+", "z-"):
                     free[link] = max(now, free[link]) + size / rate
                 if name[0] == "back":
-                    later(max(free["z+"], free["z-"]) + 3.0, ("flag", ("ex3",)))
+                    later(max(free["z+"], free["z-"]) + EX[2], ("flag", ("ex3",)))
             if name[0] == "ends":
-                later(max(free["z+"], free["z-"], now) + 3.0, ("flag", ("ex1",)))
+                later(max(free["z+"], free["z-"], now) + EX[0], ("flag", ("ex1",)))
             if name[0] == "prefix":
-                later(now + 4.0, ("flag", ("ex2",)))
+                later(now + EX[1], ("flag", ("ex2",)))
             continue
         if not events:
             raise ValueError("stuck")
@@ -393,21 +398,24 @@
     def tok_piece(dx, k, p):
         return tok.at[lax.rem(x + dx + NX, NX), half[k], own_cols if p == 0 else sib_cols]
 
-    def tok_in_here(k):
-        if k == 0:
-
-            @pl.when(home)
-            def _():
-                loads["tok"].wait()
-
-        arrived_if(away, tok_piece(0, k, 0), t_recv.at[12 + k])
-        arrived(tok_piece(0, k, 1), t_recv.at[14 + k])
+    def tok_spread(condition, k):
         for p in (0, 1):
             piece = tok_piece(0, k, p)
-            push(piece, piece, t_send.at[k * 2 + p], t_recv.at[k * 2 + p], plus)
+            push_if(condition, piece, piece, t_send.at[k * 2 + p], t_recv.at[k * 2 + p], plus)
         for p in (1, 0):
             piece = tok_piece(0, k, p)
-            push(piece, piece, t_send.at[4 + k * 2 + p], t_recv.at[4 + k * 2 + p], minus)
+            push_if(condition, piece, piece, t_send.at[4 + k * 2 + p], t_recv.at[4 + k * 2 + p], minus)
+
+    def tok_in_home(k):
+        if k == 0:
+            pl.when(home)(loads["tok"].wait)
+        arrived_if(home, tok_piece(0, k, 1), t_recv.at[14 + k])
+        tok_spread(home, k)
+
+    def tok_in_away(k):
+        arrived_if(away, tok_piece(0, k, 0), t_recv.at[12 + k])
+        arrived_if(away, tok_piece(0, k, 1), t_recv.at[14 + k])
+        tok_spread(away, k)
 
     def tok_relay(dx, k, p):
         piece = tok_piece(dx, k, p)
@@ -457,9 +465,7 @@
         halo.start()
         pl.when(away)(rest.start)
 
-    def mats():
-        all_here((0, 1))
-
+    def mats(second):
         def one(i, carry):
             tile = lax.rem(i + 4, 5)
 
@@ -472,14 +478,28 @@
             halo_out[tile] = value[ROWS - 16 :, :]
             return carry
 
-        lax.fori_loop(0, 5, one, 0)
-        for tile in range(5):
+        if second:
+            value = project(wc, 512, 512)
+            for tile in (2, 3):
+                part_of = value[:, (tile - 2) * 256 : (tile - 1) * 256]
+                ch[lent, tile] = part_of
+                halo_out[tile] = part_of[ROWS - 16 :, :]
+        else:
+            lax.fori_loop(0, 3, one, 0)
+        tiles = (2, 3) if second else (4, 0, 1)
+        for tile in tiles:
             halo, rest = channel_copies(tile)
             sent.append(halo)
             sent_if.append((away, rest))
-        pending.append(lambda: send_channels(3))
+
+        def go():
+            for tile in (2, 3) if second else (1,):
+                send_channels(tile)
+
+        pending.append(go)
 
     def dt():
+        all_here((0, 1))
         raw[lent, 0] = dot_nt(wd[...], xn[...])
         pending.append(lambda: ship(raw, 0, 5))
 
@@ -669,7 +689,7 @@
         squares[0] = squares[0] + jnp.sum(gated * gated, axis=1, keepdims=True)
 
     steps = {
-        "begin": begin, "ring": ring, "tin": tok_in_here, "tr": tok_relay, "ta": tok_far, "norm": norm, "mats": mats,
+        "begin": begin, "ring": ring, "tinh": tok_in_home, "tin": tok_in_away, "tr": tok_relay, "ta": tok_far, "norm": norm, "mats": mats,
         "dt": dt, "gmats": gmats, "chan": chan, "prep": prep, "conv": conv, "state": end_states, "inner": inner,
         "ends": ends, "prefix": prefix, "back": back, "carry": carry, "gate": gate,
     }
@@ -690,9 +710,9 @@
     lax.fori_loop(0, 8, norm_tile, 0)
     wo_load.wait()
 
-    def term(dx, core, into):
+    def term(dx, core, into, rows=slice(None)):
         cols = pl.ds(pl.multiple_of(head_of(dx, core) * DB, DB), DB)
-        into[...] = jnp.dot(no[...], wo[:, cols], preferred_element_type=F32).astype(into.dtype)
+        into[...] = jnp.dot(no[rows, :], wo[:, cols], preferred_element_type=F32).astype(into.dtype)
 
     top, low = half
 
@@ -708,19 +728,22 @@
     def chip_sum(r, rows):
         return part[r, rows, :] + sib_in[r, rows, :].astype(F32)
 
-    to_sibling(2)
-    keep(2)
-    send_sibling(2)
+    for k, rows in enumerate(half):
+        term(2, 1 - c, sib_out.at[2, rows, :], rows)
+        term(2, c, part.at[2, rows, :], rows)
+        push(sib_out.at[2, rows, :], sib_in.at[2, rows, :], o_send.at[2 + 2 * k], o_recv.at[2 + 2 * k], sibling)
     to_sibling(1)
+    arrived(sib_in.at[2, top, :], o_recv.at[2])
+    far_out[top, :] = chip_sum(2, top).astype(BF16)
+    arrived(sib_in.at[2, low, :], o_recv.at[4])
+    far_out[low, :] = chip_sum(2, low).astype(BF16)
+    push(far_out.at[top, :], far_in.at[0], x_send.at[0], x_recv.at[0], plus)
+    send_sibling(1)
     to_sibling(3)
-    send_sibling(1)
+    push(far_out.at[low, :], far_in.at[1], x_send.at[1], x_recv.at[1], minus)
     keep(1)
     send_sibling(3)
-    arrived(sib_in.at[2], o_recv.at[2])
-    far_out[...] = chip_sum(2, slice(None)).astype(BF16)
     keep(3)
-    push(far_out.at[top, :], far_in.at[0], x_send.at[0], x_recv.at[0], plus)
-    push(far_out.at[low, :], far_in.at[1], x_send.at[1], x_recv.at[1], minus)
     arrived(sib_in.at[1], o_recv.at[1])
     near_out[0, low, :] = chip_sum(1, low).astype(BF16)
     arrived(sib_in.at[3], o_recv.at[3])
@@ -772,7 +795,7 @@
         dma((6,)), dma((8, 16)), dma((8, 16)), dma((3, 4)), dma((2, 4)), dma((6, 16)), dma((6, 16)),
         dma((16,)), dma((16,)), dma((10,)), dma((10,)), dma((5,)), dma((5,)),
         dma((2, NZ)), dma((2, NZ)), dma((2, NY)), dma((2, NY)), dma((NZ,)), dma((NZ,)),
-        dma((4,)), dma((4,)), dma((6,)), dma((6,)),
+        dma((5,)), dma((5,)), dma((6,)), dma((6,)),
     ]
     return pl.pallas_call(
         kernel,

time: 129 us -> 127 us (0.984); the launches traced: 129 us -> 124 us
  Pallas kernels: 128 us -> 123 us
    pallas_call x1, Pallas kernels: 128 us -> 123 us  [body(): pl.pallas_call(kernel, out_shape=jax.ShapeDtypeStruct((ROWS, DB), BF16),...]
where the time goes in v3:
time: 127 us; the launch traced here: 124 us
  Pallas kernels  123 us (97%)
  local copies, waits for them, and re-layouts  1.77 us (1%)
    pallas_call x1, Pallas kernels, body(): pl.pallas_call(kernel, out_shape=jax.ShapeDtypeStruct((ROWS, DB), BF16),...  123 us

profile of v3, /device:TPU:24, one launch (start us, length us, event | category | flops | bytes accessed | tf_op | source)
XLA Modules:
  0.0 124.3 jit_solution(14433726594410780379)
XLA Ops:
  0.0 122.5 %shard_map.109 = bf16[384,512]{1,0:T(8,128)(2,1)} custom-call(bf16[384,512]{1,0:T(8,128)(2,1)} %tok_in.1, bf16[128,2304]{1,0:T(8,128)(2,1)} %bitcast.8, bf16[16,128]{1,0:T(8,128)(2,1)} %bitcast.10, bf16[1024,4096]{1,0:T(8,128)(2,1)} %bitcast.7, f32[1,4096]{1,0:T(1,128)} %bitcast.9, f32[1,16]{1,0:T(1,128)} %bitcast.11, f32[1,16]{1,0:T(1,128)} %bitcast.12, ...), custom_call_target="tpu_custom_call" | custom-call | tf_op jit(solution)/shard_map/pallas_call | solution.py:800
  122.5 1.8 %copy.13 = bf16[384,512]{1,0:T(8,128)(2,1)} copy(bf16[384,512]{1,0:T(8,128)(2,1)} %shard_map.109) | data formatting | bytes 786432

commit v4 on v3

--- a/solution.py
+++ b/solution.py
@@ -660,7 +660,7 @@
         sin[z] = back_out[z]
 
         def go():
-            for k in range(1, NZ):
+            for k in (4, 3, 5, 2, 6, 1, 7):
                 peer = lax.rem(z + k, NZ)
                 push(back_out.at[peer], sin.at[z], b_send.at[k], b_recv.at[k], z_peers[k - 1])
 

time: 127 us -> 127 us (level)
  no operation moved by 1% of the time
where the time goes in v4:
time: 127 us; the launch traced here: 125 us
  Pallas kernels  123 us (97%)
  local copies, waits for them, and re-layouts  1.77 us (1%)
    pallas_call x1, Pallas kernels, body(): pl.pallas_call(kernel, out_shape=jax.ShapeDtypeStruct((ROWS, DB), BF16),...  123 us

profile of v4, /device:TPU:24, one launch (start us, length us, event | category | flops | bytes accessed | tf_op | source)
XLA Modules:
  0.0 124.9 jit_solution(7379263619095588442)
XLA Ops:
  0.0 123.1 %shard_map.109 = bf16[384,512]{1,0:T(8,128)(2,1)} custom-call(bf16[384,512]{1,0:T(8,128)(2,1)} %tok_in.1, bf16[128,2304]{1,0:T(8,128)(2,1)} %bitcast.8, bf16[16,128]{1,0:T(8,128)(2,1)} %bitcast.10, bf16[1024,4096]{1,0:T(8,128)(2,1)} %bitcast.7, f32[1,4096]{1,0:T(1,128)} %bitcast.9, f32[1,16]{1,0:T(1,128)} %bitcast.11, f32[1,16]{1,0:T(1,128)} %bitcast.12, ...), custom_call_target="tpu_custom_call" | custom-call | tf_op jit(solution)/shard_map/pallas_call | solution.py:800
  123.1 1.8 %copy.13 = bf16[384,512]{1,0:T(8,128)(2,1)} copy(bf16[384,512]{1,0:T(8,128)(2,1)} %shard_map.109) | data formatting | bytes 786432
